TPU v7x, 32 devices: a whole 2x2x4 slice. The times are simulated.
32 devices in a mesh: tp: 4 (over z), fsdp: 8 (over y, x, core).
Axes of the slice: x: 2, y: 2, z: 4, core: 2. Of those that a mesh axis runs over, the one named last changes fastest.
Arguments:
- g_qkv: float32 [8, 1, 1408, 4224], P('fsdp', None, None, 'tp')
- g_out: float32 [8, 1, 1408, 1408], P('fsdp', None, None, 'tp')
- g_up: float32 [8, 1, 1408, 6144], P('fsdp', None, None, 'tp')
- g_down: float32 [8, 1, 6144, 1408], P('fsdp', None, None, 'tp')
- g_vec: float32 [8, 1, 18816], P('fsdp', None, 'tp')
- w_qkv: float32 [1, 1408, 4224], P(None, 'fsdp', 'tp')
- w_out: float32 [1, 1408, 1408], P(None, 'fsdp', 'tp')
- w_up: float32 [1, 1408, 6144], P(None, 'fsdp', 'tp')
- w_down: float32 [1, 6144, 1408], P(None, 'fsdp', 'tp')
- w_vec: float32 [1, 18816], P(None, 'tp')
- m_qkv: bfloat16 [1, 1408, 4224], P(None, 'fsdp', 'tp')
- m_out: bfloat16 [1, 1408, 1408], P(None, 'fsdp', 'tp')
- m_up: bfloat16 [1, 1408, 6144], P(None, 'fsdp', 'tp')
- m_down: bfloat16 [1, 6144, 1408], P(None, 'fsdp', 'tp')
- m_vec: bfloat16 [1, 18816], P(None, 'tp')
- vr_qkv: float32 [1, 1408], P(None, 'fsdp')
- vc_qkv: float32 [1, 4224], P(None, 'tp')
- vr_out: float32 [1, 1408], P(None, 'fsdp')
- vc_out: float32 [1, 1408], P(None, 'tp')
- vr_up: float32 [1, 1408], P(None, 'fsdp')
- vc_up: float32 [1, 6144], P(None, 'tp')
- vr_down: float32 [1, 6144], P(None, 'fsdp')
- vc_down: float32 [1, 1408], P(None, 'tp')
- v_vec: float32 [1, 18816], P(None, 'tp')
Outputs:
- output 1: float32 [1, 1408, 4224], P(None, 'fsdp', 'tp')
- output 2: float32 [1, 1408, 1408], P(None, 'fsdp', 'tp')
- output 3: float32 [1, 1408, 6144], P(None, 'fsdp', 'tp')
- output 4: float32 [1, 6144, 1408], P(None, 'fsdp', 'tp')
- output 5: float32 [1, 18816], P(None, 'tp')
- output 6: bfloat16 [1, 1408, 4224], P(None, 'fsdp', 'tp')
- output 7: bfloat16 [1, 1408, 1408], P(None, 'fsdp', 'tp')
- output 8: bfloat16 [1, 1408, 6144], P(None, 'fsdp', 'tp')
- output 9: bfloat16 [1, 6144, 1408], P(None, 'fsdp', 'tp')
- output 10: bfloat16 [1, 18816], P(None, 'tp')
- output 11: float32 [1, 1408], P(None, 'fsdp')
- output 12: float32 [1, 4224], P(None, 'tp')
- output 13: float32 [1, 1408], P(None, 'fsdp')
- output 14: float32 [1, 1408], P(None, 'tp')
- output 15: float32 [1, 1408], P(None, 'fsdp')
- output 16: float32 [1, 6144], P(None, 'tp')
- output 17: float32 [1, 6144], P(None, 'fsdp')
- output 18: float32 [1, 1408], P(None, 'tp')
- output 19: float32 [1, 18816], P(None, 'tp')
All inputs are finite; a program needn't handle non-finite values.
Results may differ from a plain program's by a relative error of at most 0.001.
Values sent between devices are 32-bit elements.
A program may use at most 1 GiB of HBM per device.

v0:
```python
import jax
import jax.numpy as jnp
from jax import lax
from jax.sharding import PartitionSpec as P, NamedSharding

TRAIN_STEP = 3
LEARN_RATE = 0.0008
WEIGHT_DECAY = 0.03
MOMENTUM = 0.9
EPSILON = 1e-30
BETA_TWO = 1.0 - TRAIN_STEP ** -0.8


def finish_step(update_val, weight, moment):
    moment_new = (MOMENTUM * moment.astype(jnp.float32) + (1.0 - MOMENTUM) * update_val).astype(jnp.bfloat16)
    weight_new = weight - LEARN_RATE * (moment_new.astype(jnp.float32) + WEIGHT_DECAY * weight)
    return weight_new, moment_new


def solution(mesh):
    fsdp_size = mesh.shape['fsdp']
    tp_size = mesh.shape['tp']

    def matrix_step(grad_shard, clip_scale, weight, moment, row_var, col_var):
        row_count = grad_shard.shape[1] * fsdp_size
        col_count = grad_shard.shape[2] * tp_size
        grad_val = grad_shard * clip_scale
        grad_sq = jnp.square(grad_val) + EPSILON
        row_sum = lax.psum(jnp.sum(grad_sq, axis=2), 'tp')
        col_sum = lax.psum(jnp.sum(grad_sq, axis=1), 'fsdp')
        row_new = BETA_TWO * row_var + (1.0 - BETA_TWO) * (row_sum / col_count)
        col_new = BETA_TWO * col_var + (1.0 - BETA_TWO) * (col_sum / row_count)
        row_mean = lax.psum(jnp.sum(row_new, axis=1, keepdims=True), 'fsdp') / row_count
        row_norm = row_new / row_mean
        update_val = grad_val / jnp.sqrt(row_norm[:, :, None] * col_new[:, None, :])
        update_sq = lax.psum(jnp.sum(jnp.square(update_val), axis=(1, 2)), ('tp', 'fsdp'))
        update_rms = jnp.sqrt(update_sq / (row_count * col_count))
        update_val = update_val / jnp.maximum(1.0, update_rms)[:, None, None]
        weight_new, moment_new = finish_step(update_val, weight, moment)
        return weight_new, moment_new, row_new, col_new

    def vector_step(grad_shard, clip_scale, weight, moment, var_old):
        vec_count = grad_shard.shape[1] * tp_size
        grad_val = grad_shard * clip_scale
        var_new = BETA_TWO * var_old + (1.0 - BETA_TWO) * (jnp.square(grad_val) + EPSILON)
        update_val = grad_val / jnp.sqrt(var_new)
        update_sq = lax.psum(jnp.sum(jnp.square(update_val), axis=1, keepdims=True), 'tp')
        update_rms = jnp.sqrt(update_sq / vec_count)
        update_val = update_val / jnp.maximum(1.0, update_rms)
        weight_new, moment_new = finish_step(update_val, weight, moment)
        return weight_new, moment_new, var_new

    def local_step(g_qkv, g_out, g_up, g_down, g_vec, w_qkv, w_out, w_up, w_down, w_vec, m_qkv, m_out, m_up, m_down, m_vec, vr_qkv, vc_qkv, vr_out, vc_out, vr_up, vc_up, vr_down, vc_down, v_vec):
        grad_shards = [lax.psum_scatter(g_part[0], 'fsdp', scatter_dimension=1, tiled=True) for g_part in (g_qkv, g_out, g_up, g_down)]
        vec_grad = lax.psum(g_vec[0], 'fsdp')
        mat_sq = sum([jnp.sum(jnp.square(g_shard)) for g_shard in grad_shards])
        total_sq = lax.psum(mat_sq, ('tp', 'fsdp')) + lax.psum(jnp.sum(jnp.square(vec_grad)), 'tp')
        clip_scale = jnp.minimum(1.0, 1.0 / jnp.sqrt(total_sq))
        weights = (w_qkv, w_out, w_up, w_down)
        moments = (m_qkv, m_out, m_up, m_down)
        row_vars = (vr_qkv, vr_out, vr_up, vr_down)
        col_vars = (vc_qkv, vc_out, vc_up, vc_down)
        results = [matrix_step(grad_shards[mat_index], clip_scale, weights[mat_index], moments[mat_index], row_vars[mat_index], col_vars[mat_index]) for mat_index in range(4)]
        vec_res = vector_step(vec_grad, clip_scale, w_vec, m_vec, v_vec)
        return (results[0][0], results[1][0], results[2][0], results[3][0], vec_res[0], results[0][1], results[1][1], results[2][1], results[3][1], vec_res[1], results[0][2], results[0][3], results[1][2], results[1][3], results[2][2], results[2][3], results[3][2], results[3][3], vec_res[2])

    grad_spec = P('fsdp', None, None, 'tp')
    vec_grad_spec = P('fsdp', None, 'tp')
    mat_spec = P(None, 'fsdp', 'tp')
    vec_spec = P(None, 'tp')
    row_spec = P(None, 'fsdp')
    col_spec = P(None, 'tp')
    state_specs = (mat_spec,) * 4 + (vec_spec,) + (mat_spec,) * 4 + (vec_spec,) + (row_spec, col_spec) * 4 + (vec_spec,)
    arg_specs = (grad_spec,) * 4 + (vec_grad_spec,) + state_specs
    return jax.shard_map(local_step, mesh=mesh, in_specs=arg_specs, out_specs=state_specs, check_vma=False)
```

profile of v0, /device:TPU:0, one launch (start us, length us, event | category | flops | bytes accessed | tf_op | source)
XLA Modules:
  0.0 430.9 jit_solution(7552148623971839052)
XLA Ops:
  7.2 3.0 copy.44
  10.3 7.2 %copy.43 = f32[1,1,1408,1056]{3,2,1,0:T(8,128)} copy(f32[1,1,1408,1056]{2,3,1,0:T(8,128)} %param.24) | data formatting | bytes 11894784 | tf_op args[0]
  17.6 0.7 reduce-scatter.9.cloned.1.call-update
  19.1 25.8 %psum.141 = f32[1,4704]{1,0:T(1,128)S(1)} all-reduce(f32[1,4704]{1,0:T(1,128)S(1)} %bitcast.33), channel_id=1, replica_groups=mesh['tp'=4,'fsdp'=8] {'fsdp'}, use_global_device_ids=true, to_apply=%region_9.0 | all-reduce | flops 4704 | bytes 37632 | tf_op jit(solution)/shard_map/psum | solution.py:55
  44.9 0.6 multiply_reduce_fusion.9
  45.5 10.1 %reduce-scatter.7.cloned.1.call-done = f32[1,176,352]{2,1,0:T(8,128)} async-done(((f32[1,1408,352]{2,1,0:T(8,128)}), f32[1,176,352]{2,1,0:T(8,128)}) %reduce-scatter.7.cloned.1.call-update) | async-done | bytes 247824 | tf_op jit(solution)/shard_map/reduce_scatter | solution.py:54
  55.6 1.6 multiply_reduce_fusion.7
  57.2 63.9 %reduce-scatter.5.cloned.1.call-done = f32[1,176,1056]{2,1,0:T(8,128)} async-done(((f32[1,1408,1056]{2,1,0:T(8,128)}), f32[1,176,1056]{2,1,0:T(8,128)}) %reduce-scatter.5.cloned.1.call-update) | async-done | bytes 743440 | tf_op jit(solution)/shard_map/reduce_scatter | solution.py:54
  121.1 2.0 multiply_reduce_fusion.5
  124.3 72.3 %reduce-scatter.9.cloned.1.call-done = f32[1,176,1536]{2,1,0:T(8,128)} async-done(((f32[1,1408,1536]{2,1,0:T(8,128)}), f32[1,176,1536]{2,1,0:T(8,128)}) %reduce-scatter.9.cloned.1.call-update) | async-done | bytes 1081360 | tf_op jit(solution)/shard_map/reduce_scatter | solution.py:54
  196.6 2.2 multiply_reduce_fusion.3
  199.4 72.5 %reduce-scatter.11.cloned.1.call-done = f32[1,768,352]{1,2,0:T(8,128)} async-done(((f32[1,6144,352]{1,2,0:T(8,128)}), f32[1,768,352]{1,2,0:T(8,128)}) %reduce-scatter.11.cloned.1.call-update) | async-done | bytes 1081360 | tf_op jit(solution)/shard_map/reduce_scatter | solution.py:54
  272.0 2.3 multiply_reduce_fusion.2
  274.9 12.3 %psum.142 = f32[]{:T(128)} all-reduce(f32[]{:T(128)} %multiply_reduce_fusion.9), channel_id=1, replica_groups=mesh['tp'=4,'fsdp'=8] {'tp'}, use_global_device_ids=true, to_apply=%region_11.0 | all-reduce | flops 1 | bytes 8 | tf_op jit(solution)/shard_map/psum | solution.py:57
  287.2 36.8 %psum.140 = f32[]{:T(128)} all-reduce(f32[]{:T(128)S(6)} %add.149), channel_id=1, replica_groups=mesh['tp'=4,'fsdp'=8] {'tp','fsdp'}, use_global_device_ids=true, to_apply=%region_8.0 | all-reduce | flops 1 | bytes 8 | tf_op jit(solution)/shard_map/psum | solution.py:57
  325.7 1.3 multiply_reduce_fusion.8
  327.8 12.0 %all-reduce.2 = (f32[1,176]{1,0:T(1,128)S(1)}, f32[1,176]{1,0:T(1,128)S(1)}, f32[1,176]{1,0:T(1,128)S(1)}, f32[1,768]{1,0:T(1,128)S(1)}, f32[1,1]{1,0:T(1,128)}) all-reduce(f32[1,176]{1,0:T(1,128)S(1)} %bitcast.42, f32[1,176]{1,0:T(1,128)S(1)} %bitcast.40, f32[1,176]{1,0:T(1,128)S(1)} %bitcast.41, ...), channel_id=1, replica_groups=mesh['tp'=4,'fsdp'=8] {'tp'}, use_global_device_ids=true, to_apply=%region_13.0 | all-reduce | flops 1297 | bytes 10376 | tf_op jit(solution)/shard_map/psum | solution.py:29
  339.8 0.6 fusion.12
  340.4 0.6 fusion.14
  342.2 24.3 %all-reduce.1 = (f32[1,1056]{1,0:T(1,128)S(1)}, f32[1,1]{1,0:T(1,128)}, f32[1,352]{1,0:T(1,128)S(1)}, f32[1,1]{1,0:T(1,128)}, f32[1,1536]{1,0:T(1,128)S(1)}, /*i...) all-reduce(f32[1,1056]{1,0:T(1,128)S(1)} %reduce_sum.231, ...), channel_id=1, replica_groups=mesh['tp'=4,'fsdp'=8] {'fsdp'}, use_global_device_ids=true, to_apply=%region_17.0 | all-reduce | flops 3300 | bytes 26400 | tf_op jit(solution)/shard_map/psum | solution.py:30
  369.1 0.6 fusion.9
  369.7 0.6 fusion.11
  370.9 1.1 multiply_reduce_fusion
  372.0 1.1 multiply_reduce_fusion.1
  373.1 0.8 multiply_reduce_fusion.6
  373.9 1.0 multiply_reduce_fusion.4
  374.8 37.7 %all-reduce = (f32[1]{0:T(128)}, f32[1]{0:T(128)}, f32[1]{0:T(128)}, f32[1]{0:T(128)}) all-reduce(f32[1]{0:T(128)} %bitcast.9, f32[1]{0:T(128)} %bitcast.15, f32[1]{0:T(128)} %bitcast.21, f32[1]{0:T(128)} %bitcast.25), channel_id=1, replica_groups=mesh['tp'=4,'fsdp'=8] {'tp','fsdp'}, use_global_device_ids=true, to_apply=%region_19.0 | all-reduce | flops 4 | bytes 32 | tf_op jit(solution)/shard_map/psum | solution.py:36
  416.0 0.7 multiply_subtract_fusion.4
  416.7 3.2 multiply_subtract_fusion
  419.9 1.7 multiply_subtract_fusion.1
  421.7 0.9 multiply_subtract_fusion.3
  422.9 1.5 multiply_subtract_fusion.2
  (75 shorter events, 4.1 us)
Async XLA Ops:
  7.2 48.4 %reduce-scatter.7.cloned.1.call-start = ((), (), s32[]{:S(2)}) async-start(), calls=%async_computation.5 | async-start | bytes 2433024 | tf_op jit(solution)/shard_map/reduce_scatter | solution.py:54
  10.3 110.8 %reduce-scatter.5.cloned.1.call-start = ((), (), s32[]{:S(2)}) async-start(), calls=%async_computation.4 | async-start | bytes 7299072 | tf_op jit(solution)/shard_map/reduce_scatter | solution.py:54
  17.6 179.1 %reduce-scatter.9.cloned.1.call-start = ((), (), s32[]{:S(2)}) async-start(), calls=%async_computation.6 | async-start | bytes 9732096 | tf_op jit(solution)/shard_map/reduce_scatter | solution.py:54
  18.3 253.7 %reduce-scatter.11.cloned.1.call-start = ((), (), s32[]{:S(2)}) async-start(), calls=%async_computation.7 | async-start | bytes 9732096 | tf_op jit(solution)/shard_map/reduce_scatter | solution.py:54
  18.3 0.7 copy-start.10
  196.6 130.3 %copy-start.3 = (f32[1,176,352]{2,1,0:T(8,128)S(1)}, f32[1,176,352]{2,1,0:T(8,128)}, u32[]{:S(2)}) copy-start(f32[1,176,352]{2,1,0:T(8,128)} %reduce-scatter.7.cloned.1.call-done) | copy-start | bytes 743428
  272.0 53.4 %copy-start = (f32[1,768,352]{1,2,0:T(8,128)S(1)}, f32[1,768,352]{1,2,0:T(8,128)}, u32[]{:S(2)}) copy-start(f32[1,768,352]{1,2,0:T(8,128)} %reduce-scatter.11.cloned.1.call-done) | copy-start | bytes 3244036
  272.0 53.7 %copy-start.11 = (f32[1,4704]{1,0:T(1,128)S(1)}, f32[1,4704]{1,0:T(1,128)}, u32[]{:S(2)}) copy-start(f32[1,4704]{1,0:T(1,128)} %param.47) | copy-start | bytes 56452
  272.0 55.2 %copy-start.1 = (f32[1,176,1536]{2,1,0:T(8,128)S(1)}, f32[1,176,1536]{2,1,0:T(8,128)}, u32[]{:S(2)}) copy-start(f32[1,176,1536]{2,1,0:T(8,128)} %reduce-scatter.9.cloned.1.call-done) | copy-start | bytes 3244036
  325.4 2.1 copy-start.2
  326.9 12.8 %copy-start.20 = (f32[1,768]{1,0:T(1,128)S(1)}, f32[1,768]{1,0:T(1,128)}, u32[]{:S(2)}) copy-start(f32[1,768]{1,0:T(1,128)} %param.45) | copy-start | bytes 9220
  326.9 13.4 %copy-start.23 = (f32[1,176]{1,0:T(1,128)S(1)}, f32[1,176]{1,0:T(1,128)}, u32[]{:S(2)}) copy-start(f32[1,176]{1,0:T(1,128)} %param.41) | copy-start | bytes 2116
  326.9 14.0 %copy-start.24 = (f32[1,176]{1,0:T(1,128)S(1)}, f32[1,176]{1,0:T(1,128)}, u32[]{:S(2)}) copy-start(f32[1,176]{1,0:T(1,128)} %param.43) | copy-start | bytes 2116
  326.9 14.6 %copy-start.25 = (f32[1,176]{1,0:T(1,128)S(1)}, f32[1,176]{1,0:T(1,128)}, u32[]{:S(2)}) copy-start(f32[1,176]{1,0:T(1,128)} %param.39) | copy-start | bytes 2116
  327.1 42.0 %copy-start.15 = (f32[1,1536]{1,0:T(1,128)S(1)}, f32[1,1536]{1,0:T(1,128)}, u32[]{:S(2)}) copy-start(f32[1,1536]{1,0:T(1,128)} %param.44) | copy-start | bytes 18436
  327.1 42.6 %copy-start.16 = (f32[1,1056]{1,0:T(1,128)S(1)}, f32[1,1056]{1,0:T(1,128)}, u32[]{:S(2)}) copy-start(f32[1,1056]{1,0:T(1,128)} %param.40) | copy-start | bytes 12676
  327.1 43.2 %copy-start.21 = (f32[1,352]{1,0:T(1,128)S(1)}, f32[1,352]{1,0:T(1,128)}, u32[]{:S(2)}) copy-start(f32[1,352]{1,0:T(1,128)} %param.46) | copy-start | bytes 4228
  327.1 43.2 %copy-start.22 = (f32[1,352]{1,0:T(1,128)S(1)}, f32[1,352]{1,0:T(1,128)}, u32[]{:S(2)}) copy-start(f32[1,352]{1,0:T(1,128)} %param.42) | copy-start | bytes 4228
  340.4 32.7 %copy-start.14 = (f32[1,768]{1,0:T(1,128)}, f32[1,768]{1,0:T(1,128)S(1)}, u32[]{:S(2)}) copy-start(f32[1,768]{1,0:T(1,128)S(1)} %get-tuple-element.63) | copy-start | bytes 9220
  341.0 32.1 %copy-start.17 = (f32[1,176]{1,0:T(1,128)}, f32[1,176]{1,0:T(1,128)S(1)}, u32[]{:S(2)}) copy-start(f32[1,176]{1,0:T(1,128)S(1)} %get-tuple-element.67) | copy-start | bytes 2116
  341.6 31.5 %copy-start.18 = (f32[1,176]{1,0:T(1,128)}, f32[1,176]{1,0:T(1,128)S(1)}, u32[]{:S(2)}) copy-start(f32[1,176]{1,0:T(1,128)S(1)} %get-tuple-element.65) | copy-start | bytes 2116
  342.2 30.9 %copy-start.19 = (f32[1,176]{1,0:T(1,128)}, f32[1,176]{1,0:T(1,128)S(1)}, u32[]{:S(2)}) copy-start(f32[1,176]{1,0:T(1,128)S(1)} %get-tuple-element.69) | copy-start | bytes 2116
  372.0 44.0 %copy-start.12 = (f32[1,4704]{1,0:T(1,128)S(1)}, f32[1,4704]{1,0:T(1,128)}, u32[]{:S(2)}) copy-start(f32[1,4704]{1,0:T(1,128)} %param.33) | copy-start | bytes 56452
  372.0 44.0 %copy-start.13 = (bf16[1,4704]{1,0:T(2,128)(2,1)S(1)}, bf16[1,4704]{1,0:T(2,128)(2,1)}, u32[]{:S(2)}) copy-start(bf16[1,4704]{1,0:T(2,128)(2,1)} %param.38) | copy-start | bytes 28228
  416.7 3.2 copy-start.4
  416.7 3.2 copy-start.6
  419.9 1.8 copy-start.8
  419.9 1.8 copy-start.9
  419.9 2.7 copy-start.7
  421.7 1.2 copy-start.5
Sparse Core Ops, SparseCore 0:
  11.3 44.1 reduce-scatter.6
  59.0 62.0 reduce-scatter.4
  124.6 71.9 reduce-scatter.8
  200.0 71.9 reduce-scatter.10
where the time goes:
time: 432 us; the launch traced here: 431 us
  waiting for transfers between devices  220 us (51%)
  blocking collectives  149 us (34%)
  other arithmetic  27 us (6%)
  between operations  24 us (6%)
  local copies, waits for them, and re-layouts  10.8 us (2%)
    reduce_scatter x4, waiting for transfers between devices, local_step(): lax.psum_scatter(g_part[0], 'fsdp', scatter_dimension=1, tiled=True)  219 us
    psum x1, blocking collectives, matrix_step(): lax.psum(jnp.sum(jnp.square(update_val), axis=(1, 2)), ('tp', 'fsdp'))  37.7 us
    psum x1, blocking collectives, local_step(): lax.psum(mat_sq, ('tp', 'fsdp'))  36.8 us
    psum x1, blocking collectives, local_step(): vec_grad = lax.psum(g_vec[0], 'fsdp')  25.8 us
    psum x1, blocking collectives, matrix_step(): col_sum = lax.psum(jnp.sum(grad_sq, axis=1), 'fsdp')  24.3 us
    psum x1, blocking collectives, local_step(): lax.psum(jnp.sum(jnp.square(vec_grad)), 'tp')  12.3 us
    psum x1, blocking collectives, matrix_step(): row_sum = lax.psum(jnp.sum(grad_sq, axis=2), 'tp')  12 us
    unnamed x54, local copies, waits for them, and re-layouts  10.8 us
  transfers between devices with their start and end apart: 4, of which 4 were waited for; matrix products, arithmetic and copies ran while one was open for 3% of the time, Pallas kernels for 0%

commit v1 on v0

v1 whole, which is shorter than its diff:
```python
import jax
import jax.numpy as jnp
from jax import lax
from jax.experimental import pallas as pl
from jax.experimental.pallas import tpu as pltpu
from jax.sharding import PartitionSpec as P

TRAIN_STEP = 3
LEARN_RATE = 0.0008
WEIGHT_DECAY = 0.03
MOMENTUM = 0.9
EPSILON = 1e-30
BETA_TWO = 1.0 - TRAIN_STEP ** -0.8
KEEP, MIX = BETA_TWO, 1.0 - BETA_TWO

F32 = jnp.float32
BF16 = jnp.bfloat16
MESH = pl.DeviceIdType.MESH
HIGHEST = lax.Precision.HIGHEST
TP, FSDP, DEVICES = 4, 8, 32
SUB, LANE = 8, 128

ROWS = (176, 176, 176, 768)
COLS = (1056, 352, 1536, 352)
VEC = 4704
R, QO, UP, DR, DC = ROWS[0], COLS[0] + COLS[1], COLS[2], ROWS[3], COLS[3]
HALF_R, HALF_DC = R // 2, DC // 2
STEPS = QO // LANE
D_STEP = HALF_DC // STEPS
Q_FULL = COLS[0] // LANE
Q_LEFT = COLS[0] - Q_FULL * LANE
ROW_TILES = R // SUB
D_TILES = DC // SUB
WIDE = -(-(QO + UP) // (SUB * LANE)) * SUB * LANE
LOOK, SLOTS = 3, 4
U_, QO_, D_ = 0, 1, 2
VR_AT, VEC_AT = 4, 8


def lanes(shape):
    return lax.broadcasted_iota(jnp.int32, shape, len(shape) - 1)


def sublanes(shape):
    return lax.broadcasted_iota(jnp.int32, shape, len(shape) - 2)


def total(x):
    return jnp.sum(jnp.sum(x, axis=1, keepdims=True), axis=0, keepdims=True)


def pick(x, lane):
    return jnp.sum(jnp.where(lanes(x.shape) == lane, x, 0.0), axis=1, keepdims=True)


def dot(a, b):
    return lax.dot_general(a, b, (((1,), (0,)), ((), ())), precision=HIGHEST, preferred_element_type=F32)


def own_sublane(n):
    return lanes((SUB, n)) % SUB == sublanes((SUB, n))


def to_tiles(row, at):
    n = row.shape[1]
    chosen = (sublanes((n, LANE)) // SUB + at == lanes((n, LANE))).astype(F32)
    return dot(jnp.where(own_sublane(n), row, 0.0), chosen)


def from_tiles(tiles, at, n):
    chosen = (lanes((LANE, n)) // SUB + at == sublanes((LANE, n))).astype(F32)
    return jnp.sum(jnp.where(own_sublane(n), dot(tiles, chosen), 0.0), axis=0, keepdims=True)


def across(tiles, t):
    return jnp.broadcast_to(tiles[:, t:t + 1], (SUB, LANE))


def reduce_kernel(*refs):
    (gq, go, gu, gd, gv, vrq, vro, vru, vrd, vcq, vco, vcu, vcd, vv,
     hqo, hu, hd, hv, inv_out,
     n_rq, n_ro, n_ru, n_rd, n_cq, n_co, n_cu, n_cd, vv_new,
     own_qo, own_u, own_d, peer_qo, peer_u, peer_d, s_qo,
     a_qo, a_u, a_d, b_qo, b_u, b_d,
     vec_own, vec_in, vec_mid, vv_in,
     r_q, r_o, r_u, r_d, c_q, c_o, c_u, c_d,
     p_q, p_o, cs_qo, cs_u, rs_d, rp_acc, rpd_acc, rp_old, rpd_old, col_buf, rowd_buf,
     cs_all, rp_all, rsd_all, rpd_all, s_all, u_all,
     own_sem, peer_sem, push_sem, first_sem, second_sem, a_sem, b_sem,
     vec_sem, vec_send, vec_recv, small_sem, stat_send, stat_recv) = refs

    me = lax.axis_index("fsdp")
    z = lax.axis_index("tp")
    core = lax.rem(me, 2)
    x = lax.rem(me // 2, 2)
    y = me // 4
    linear = z * FSDP + me
    mate = {"fsdp": me + 1 - 2 * core}
    across_x = {"fsdp": me + 2 - 4 * x}
    across_y = {"fsdp": me + 4 - 8 * y}
    every = slice(None)

    owns, peers = (own_u, own_qo, own_d), (peer_u, peer_qo, peer_d)
    sums, firsts, seconds = (own_u, s_qo, own_d), (a_u, a_qo, a_d), (b_u, b_qo, b_d)

    def send(src, dst, ssem, rsem, to):
        return pltpu.make_async_remote_copy(
            src_ref=src, dst_ref=dst, send_sem=ssem, recv_sem=rsem,
            device_id=to, device_id_type=MESH)

    def index(kind, lead, side, k):
        if kind == QO_:
            return (k,) + lead + (pl.ds(HALF_R * side, HALF_R),)
        if kind == U_:
            return lead + (pl.ds(pl.multiple_of(HALF_R * side + SUB * k, SUB), SUB),)
        return lead + (pl.ds(pl.multiple_of(HALF_DC * side + D_STEP * k, SUB), D_STEP),)

    def whole(kind, lead, side):
        if kind == QO_:
            return (every,) + lead + (pl.ds(HALF_R * side, HALF_R),)
        n = HALF_R if kind == U_ else HALF_DC
        return lead + (pl.ds(n * side, n),)

    def first(kind, side, at, sem):
        lead, to = (((every, 1 - x), across_x), ((1 - y, every), across_y))[side]
        return send(sums[kind].at[at(kind, lead, side)], firsts[kind].at[at(kind, (every,), side)],
                    first_sem.at[kind, side], sem, to)

    def second(kind, side, at, sem):
        lead, to = (((1 - y, x), across_y), ((y, 1 - x), across_x))[side]
        return send(sums[kind].at[at(kind, lead, side)], seconds[kind].at[at(kind, (), side)],
                    second_sem.at[kind, side], sem, to)

    def chunk(k):
        return lambda kind, lead, side: index(kind, lead, side, k)

    def load(kind, k, side, away):
        if away:
            dst, sem, c = peers[kind], peer_sem.at[kind, side, k], 1 - core
            copy = lambda a, b: send(a, b, push_sem.at[kind], sem, mate)
        else:
            dst, sem, c = owns[kind], own_sem.at[kind, side, k], core
            copy = lambda a, b: pltpu.make_async_copy(a, b, sem)
        if kind == U_:
            at = index(kind, (), side, k)
            return [(None, copy(gu.at[(every, every, c) + at], dst.at[(every, every) + at]))]
        if kind == D_:
            at = index(kind, (), side, k)
            return [(None, copy(gd.at[at + (pl.ds(pl.multiple_of(DR * (2 * b + c), LANE), DR),)],
                                dst.at[(b // 2, b % 2) + at])) for b in range(4)]
        slot = dst.at[k if away else lax.rem(k, SLOTS)]
        rest = LANE - Q_LEFT
        at_q = pl.multiple_of(LANE * jnp.minimum(k, Q_FULL - 1), LANE)
        at_o = pl.multiple_of(rest + LANE * jnp.maximum(k - Q_FULL - 1, 0), SUB)
        return [(k < Q_FULL, copy(gq.at[pl.ds(at_q, LANE)], slot)),
                (k == Q_FULL, copy(gq.at[pl.ds(Q_FULL * LANE, Q_LEFT)], slot.at[pl.ds(0, Q_LEFT)])),
                (k == Q_FULL, copy(go.at[pl.ds(0, rest)], slot.at[pl.ds(Q_LEFT, rest)])),
                (k > Q_FULL, copy(go.at[pl.ds(at_o, LANE)], slot))]

    def start_kind(kind, k, away):
        for side in range(1 if kind == QO_ else 2):
            for cond, copy in load(kind, k, side, away):
                if cond is None:
                    copy.start()
                else:
                    pl.when(cond)(copy.start)

    def start_loads(step, away):
        for kind in range(3):
            k = step - kind * STEPS
            pl.when(jnp.logical_and(k >= 0, k < STEPS))(lambda kind=kind, k=k: start_kind(kind, k, away))

    def loaded(kind, side, k):
        if kind == QO_:
            here, there = own_qo.at[lax.rem(k, SLOTS)], peer_qo.at[k]
        else:
            at = index(kind, (every, every), side, k)
            here, there = owns[kind].at[at], peers[kind].at[at]
        pltpu.make_async_copy(here, here, own_sem.at[kind, side, k]).wait()
        send(there, there, push_sem.at[kind], peer_sem.at[kind, side, k], mate).wait_recv()

    smalls = [(vrq, r_q), (vro, r_o), (vru, r_u), (vrd, r_d),
              (vcq, c_q), (vco, c_o), (vcu, c_u), (vcd, c_d), (vv, vv_in)]
    small_copies = [pltpu.make_async_copy(a, b, small_sem.at[i]) for i, (a, b) in enumerate(smalls)]
    vec_copy = pltpu.make_async_copy(gv, vec_own, vec_sem.at[0])

    for step in range(LOOK):
        start_kind(U_, step, False)
    vec_copy.start()
    for copy in small_copies:
        copy.start()
    barrier = pltpu.get_barrier_semaphore()

    def other(d):
        to = lax.rem(linear + d, DEVICES)
        return {"tp": to // FSDP, "fsdp": lax.rem(to, FSDP)}

    for d in range(1, DEVICES):
        pl.semaphore_signal(barrier, inc=1, device_id=other(d), device_id_type=MESH)
    pl.semaphore_wait(barrier, DEVICES - 1)

    for step in range(LOOK):
        start_kind(U_, step, True)
    vec_copy.wait()
    vec_core = send(vec_own, vec_in.at[0], vec_send.at[0], vec_recv.at[0], mate)
    vec_x = send(vec_mid.at[0], vec_in.at[1], vec_send.at[1], vec_recv.at[1], across_x)
    vec_y = send(vec_mid.at[1], vec_in.at[2], vec_send.at[2], vec_recv.at[2], across_y)
    vec_core.start()

    def turn(k, which):
        slot = lax.rem(k, SLOTS)
        for tile in range(STEPS):
            lo = LANE * tile
            cuts = [(b, max(lo, R * (2 * b + which)), min(lo + LANE, R * (2 * b + which) + R)) for b in range(4)]
            cuts = [cut for cut in cuts if cut[1] < cut[2]]
            if cuts:
                at = (every, pl.ds(lo, LANE))
                turned = (own_qo[(slot,) + at] + peer_qo[(k,) + at]).T
                for b, start, stop in cuts:
                    first_row = start - R * (2 * b + which)
                    s_qo[k, b // 2, b % 2, pl.ds(first_row, stop - start), :] = turned[start - lo:stop - lo]

    def stage1(kind):
        def body(k, _):
            start_loads(k + kind * STEPS + LOOK, False)
            start_loads(k + kind * STEPS + LOOK, True)
            if kind == QO_:
                loaded(kind, 0, k)
                for which in range(2):
                    pl.when(core == which)(lambda which=which: turn(k, which))
            for side in range(2):
                if kind != QO_:
                    loaded(kind, side, k)
                    for b in range(4):
                        at = index(kind, (b // 2, b % 2), side, k)
                        owns[kind][at] = owns[kind][at] + peers[kind][at]
                first(kind, side, chunk(k), a_sem.at[kind, side, k]).start()
            return _
        return body

    vec_core.wait_recv()
    vec_mid[0] = vec_own[...] + vec_in[0]
    lax.fori_loop(0, 1, stage1(U_), 0)
    vec_x.start()
    lax.fori_loop(1, STEPS, stage1(U_), 0)
    for kind in (QO_, D_):
        lax.fori_loop(0, STEPS, stage1(kind), 0)

    for copy in small_copies:
        copy.wait()
    for ref in (cs_qo, cs_u, rs_d, rp_acc, rpd_acc, p_q, p_o):
        ref[...] = jnp.zeros_like(ref)
    old = to_tiles(r_q[...], 0) + to_tiles(r_o[...], ROW_TILES) + to_tiles(r_u[...], 2 * ROW_TILES)
    rp_old[...] = old
    rpd_old[...] = to_tiles(c_d[...], 0)
    lane = lanes((SUB, LANE))
    lane1 = lanes((1, LANE))
    masks = [jnp.logical_and(lane >= ROW_TILES * m, lane < ROW_TILES * (m + 1)) for m in range(3)]
    old_sums = [total(jnp.where(masks[m], old, 0.0)) for m in range(3)] + [total(r_d[...])]

    def stage2(kind):
        def body(k, _):
            for side in range(2):
                first(kind, side, chunk(k), a_sem.at[kind, side, k]).wait_recv()
                lead, mine = (((1 - y, x), 1 - y), ((y, 1 - x), 1 - x))[side]
                at = index(kind, lead, side, k)
                sums[kind][at] = sums[kind][at] + firsts[kind][index(kind, (mine,), side, k)]
                second(kind, side, chunk(k), b_sem.at[kind, side, k]).start()
            return _
        return body

    for kind in (U_, QO_):
        lax.fori_loop(0, STEPS, stage2(kind), 0)
    vec_x.wait_recv()
    vec_mid[1] = vec_mid[0] + vec_in[1]
    vec_y.start()
    lax.fori_loop(0, STEPS, stage2(D_), 0)

    def finished(kind, side, k):
        second(kind, side, chunk(k), b_sem.at[kind, side, k]).wait_recv()
        return (sums[kind][index(kind, (y, x), side, k)]
                + firsts[kind][index(kind, ((y, x)[side],), side, k)]
                + seconds[kind][index(kind, (), side, k)])

    def stage3_u(k, _):
        for side in range(2):
            full = finished(U_, side, k)
            hu[index(U_, (), side, k)] = full
            sq = full * full
            cs_u[...] += sq
            row = jnp.sum(sq, axis=1, keepdims=True)
            rp_acc[...] = jnp.where(lane == 2 * ROW_TILES + STEPS * side + k, row, rp_acc[...])
        return _

    def stage3_qo(k, _):
        for side in range(2):
            rows = pl.ds(HALF_R * side, HALF_R)
            full = finished(QO_, side, k)
            hqo[rows, pl.ds(pl.multiple_of(LANE * k, LANE), LANE)] = full
            sq = full * full
            in_q = lanes(sq.shape) + LANE * k < COLS[0]
            p_q[rows, :] += jnp.where(in_q, sq, 0.0)
            p_o[rows, :] += jnp.where(in_q, 0.0, sq)
            part = sq[:SUB]
            for t in range(1, STEPS):
                part = part + sq[SUB * t:SUB * t + SUB]
            cs_qo[k] += part
        return _

    def stage3_d(k, _):
        for side in range(2):
            full = finished(D_, side, k)
            hd[index(D_, (), side, k)] = full
            sq = full * full
            both = rpd_acc[...]
            for t in range(D_STEP // SUB):
                part = sq[SUB * t:SUB * t + SUB]
                rs_d[...] += part
                col = jnp.sum(part, axis=1, keepdims=True)
                at = (HALF_DC * side + D_STEP * k) // SUB + t
                both = jnp.where(lane == at, col, both)
            rpd_acc[...] = both
        return _

    def to_group(buf, at, i, n, axis, here):
        for d in range(1, n):
            send(buf.at[at], buf.at[at], stat_send.at[i], stat_recv.at[i],
                 {axis: lax.rem(here + d, n)}).start()

    def to_all(buf, i):
        for d in range(1, DEVICES):
            send(buf.at[linear], buf.at[linear], stat_send.at[i], stat_recv.at[i], other(d)).start()

    def spread(buf, i, n):
        part = buf.at[pl.ds(0, n - 1)]
        return send(part, part, stat_send.at[i], stat_recv.at[i], mate)

    def gathered(buf, i, n):
        spread(buf, i, n).wait_recv()
        out = buf[0]
        for d in range(1, n):
            out = out + buf[d]
        return out

    lax.fori_loop(0, STEPS, stage3_u, 0)
    lax.fori_loop(0, STEPS, stage3_qo, 0)
    vec_y.wait_recv()
    vec = vec_mid[1] + vec_in[2]
    hv[...] = vec
    rp = rp_acc[...]
    for t in range(ROW_TILES):
        for m, ref in enumerate((p_q, p_o)):
            row = jnp.sum(ref[pl.ds(SUB * t, SUB), :], axis=1, keepdims=True)
            rp = jnp.where(lane == ROW_TILES * m + t, row, rp)
    rp_all[z] = rp
    cs = [jnp.sum(cs_qo[k], axis=0, keepdims=True) for k in range(STEPS)]
    cs.append(jnp.sum(cs_u[...], axis=0, keepdims=True))
    cs_all[me] = jnp.concatenate(cs + [jnp.zeros((1, WIDE - QO - UP), F32)], axis=1)
    to_group(rp_all, z, 0, TP, "tp", z)
    to_group(cs_all, me, 1, FSDP, "fsdp", me)
    pack = jnp.where(lane1 == VEC_AT, jnp.sum(vec * vec, axis=1, keepdims=True), 0.0)
    for m in range(4):
        pack = jnp.where(lane1 == VR_AT + m, old_sums[m], pack)
    for m in range(3):
        pack = jnp.where(lane1 == m, total(jnp.where(masks[m], rp, 0.0)), pack)

    lax.fori_loop(0, STEPS, stage3_d, 0)
    rs = rs_d[...]
    s_all[linear] = jnp.where(lane1 == 3, total(rs), pack)
    to_all(s_all, 4)
    rsd_all[z] = jnp.sum(rs, axis=0, keepdims=True)
    to_group(rsd_all, z, 2, TP, "tp", z)
    rpd_all[me] = rpd_acc[...]
    to_group(rpd_all, me, 3, FSDP, "fsdp", me)

    vc_old = jnp.concatenate([c_q[...], c_o[...], c_u[...], jnp.ones((1, WIDE - QO - UP), F32)], axis=1)
    rp = gathered(rp_all, 0, TP)
    cs = gathered(cs_all, 1, FSDP)
    rsd = gathered(rsd_all, 2, TP)
    rpd = gathered(rpd_all, 3, FSDP)
    pack = gathered(s_all, 4, DEVICES)
    squares = [pick(pack, m) for m in range(4)]
    norm = jnp.sqrt((squares[0] + squares[1]) + (squares[2] + squares[3]) + pick(pack, VEC_AT) / FSDP)
    clip = jnp.minimum(1.0, 1.0 / norm)

    def clipped(v):
        return jnp.where(clip > 0.0, (v * clip) * clip, 0.0)

    means = []
    for m in range(4):
        r_all, c_all = float(ROWS[m] * FSDP), float(COLS[m] * TP)
        means.append(KEEP * (pick(pack, VR_AT + m) / (TP * r_all))
                     + MIX * (clipped(squares[m]) / (r_all * c_all) + EPSILON))
    mean_rp = jnp.where(masks[0], means[0], jnp.where(masks[1], means[1], means[2]))
    wide = jnp.where(masks[0], float(COLS[0] * TP), jnp.where(masks[1], float(COLS[1] * TP), float(COLS[2] * TP)))
    row_new = KEEP * rp_old[...] + MIX * (clipped(rp) / wide + EPSILON)
    row_sq = mean_rp / row_new
    rowd_new = KEEP * r_d[...] + MIX * (clipped(rsd) / float(DC * TP) + EPSILON)
    rowd_buf[...] = clip * jnp.sqrt(means[3] / rowd_new)
    col_new = KEEP * vc_old + MIX * (clipped(cs) / float(R * FSDP) + EPSILON)
    col_buf[...] = clip / jnp.sqrt(col_new)
    cold_new = KEEP * rpd_old[...] + MIX * (clipped(rpd) / float(DR * FSDP) + EPSILON)
    cold_sq = 1.0 / cold_new

    def tile(ref, j):
        return jnp.broadcast_to(ref[:, pl.ds(LANE * j, LANE)], (SUB, LANE))

    zero = jnp.zeros((SUB, LANE), F32)
    acc = [zero] * 4
    in_q = lane < Q_LEFT
    col_t = [tile(col_buf, j) for j in range(STEPS + UP // LANE)]
    for t in range(ROW_TILES):
        rows = pl.ds(SUB * t, SUB)
        part = [zero] * 3
        for j in range(STEPS):
            u = hqo[rows, pl.ds(LANE * j, LANE)] * col_t[j]
            u = u * u
            if j == Q_FULL:
                part[0] = part[0] + jnp.where(in_q, u, 0.0)
                part[1] = part[1] + jnp.where(in_q, 0.0, u)
            else:
                part[j // Q_FULL] = part[j // Q_FULL] + u
        for j in range(UP // LANE):
            u = hu[rows, pl.ds(LANE * j, LANE)] * col_t[STEPS + j]
            part[2] = part[2] + u * u
        for m in range(3):
            acc[m] = acc[m] + part[m] * across(row_sq, ROW_TILES * m + t)
    rowd_t = [tile(rowd_buf, j) for j in range(DR // LANE)]
    for t in range(D_TILES):
        part = zero
        for j in range(DR // LANE):
            u = hd[pl.ds(SUB * t, SUB), pl.ds(LANE * j, LANE)] * rowd_t[j]
            part = part + u * u
        acc[3] = acc[3] + part * across(cold_sq, t)
    vec = hv[...] * clip
    v_new = KEEP * vv_in[...] + MIX * (vec * vec + EPSILON)
    vec = vec / jnp.sqrt(v_new)
    pack = jnp.where(lane1 == VEC_AT, jnp.sum(vec * vec, axis=1, keepdims=True), 0.0)
    for m in range(4):
        pack = jnp.where(lane1 == m, total(acc[m]), pack)
    u_all[linear] = pack
    to_all(u_all, 5)

    vv_new[...] = v_new
    hv[...] = vec
    row = jnp.sqrt(row_sq)
    cold = jnp.sqrt(cold_sq)
    for t in range(ROW_TILES):
        rows = pl.ds(SUB * t, SUB)
        scale = [across(row, ROW_TILES * m + t) for m in range(3)]
        mixed = jnp.where(in_q, scale[0], scale[1])
        for j in range(STEPS):
            at = pl.ds(LANE * j, LANE)
            hqo[rows, at] = hqo[rows, at] * col_t[j] * (mixed if j == Q_FULL else scale[j // Q_FULL])
        for j in range(UP // LANE):
            at = pl.ds(LANE * j, LANE)
            hu[rows, at] = hu[rows, at] * col_t[STEPS + j] * scale[2]
    for t in range(D_TILES):
        rows = pl.ds(SUB * t, SUB)
        scale = across(cold, t)
        for j in range(DR // LANE):
            at = pl.ds(LANE * j, LANE)
            hd[rows, at] = hd[rows, at] * rowd_t[j] * scale
    for m, ref in enumerate((n_rq, n_ro, n_ru)):
        ref[...] = from_tiles(row_new, ROW_TILES * m, R)
    n_rd[...] = rowd_new
    n_cq[...] = col_new[:, :COLS[0]]
    n_co[...] = col_new[:, COLS[0]:QO]
    n_cu[...] = col_new[:, QO:QO + UP]
    n_cd[...] = from_tiles(cold_new, 0, DC)

    for kind in range(3):
        send(peers[kind], peers[kind], push_sem.at[kind], peer_sem.at[kind, 0, 0], mate).wait_send()
        for side in range(2):
            first(kind, side, whole, a_sem.at[kind, side, 0]).wait_send()
            second(kind, side, whole, b_sem.at[kind, side, 0]).wait_send()
    for copy in (vec_core, vec_x, vec_y):
        copy.wait_send()
    groups = ((rp_all, TP), (cs_all, FSDP), (rsd_all, TP), (rpd_all, FSDP), (s_all, DEVICES), (u_all, DEVICES))
    for i, (buf, n) in enumerate(groups):
        if i < len(groups) - 1:
            spread(buf, i, n).wait_send()

    pack = gathered(u_all, len(groups) - 1, DEVICES)
    count = jnp.full((1, LANE), float(VEC * TP * FSDP), F32)
    for m in range(4):
        count = jnp.where(lane1 == m, float(ROWS[m] * FSDP * COLS[m] * TP), count)
    inv_out[...] = 1.0 / jnp.maximum(1.0, jnp.sqrt(pack / count))
    spread(u_all, len(groups) - 1, DEVICES).wait_send()


PIECES = ((3, 0, HALF_DC), (3, HALF_DC, HALF_DC), (2, 0, R), (0, 0, R), (1, 0, R))
HELD = (ROWS[:3] + (DC,), COLS[:3] + (DR,))
GROUP = 16


def update_kernel(*refs):
    (hqo, hu, hd, hv, inv, vrq, vro, vru, vrd, vcq, vco, vcu, vcd, vv,
     wq, wo, wu, wd, wv, mq, mo, mu, md, mv,
     wq_out, wo_out, wu_out, wd_out, wv_out, mq_out, mo_out, mu_out, md_out, mv_out,
     vrq_out, vcq_out, vro_out, vco_out, vru_out, vcu_out, vrd_out, vcd_out, vv_out,
     bwq, bwo, bwu, bwd, bmq, bmo, bmu, bmd, out_sem) = refs
    held = ((hqo, 0), (hqo, COLS[0]), (hu, 0), (hd, 0))
    w_in, m_in = (wq, wo, wu, wd), (mq, mo, mu, md)
    w_buf, m_buf = (bwq, bwo, bwu, bwd), (bmq, bmo, bmu, bmd)
    w_out, m_out = (wq_out, wo_out, wu_out, wd_out), (mq_out, mo_out, mu_out, md_out)

    def finish(u, w, m):
        m_new = (MOMENTUM * m.astype(F32) + (1.0 - MOMENTUM) * u).astype(BF16)
        return w - LEARN_RATE * (m_new.astype(F32) + WEIGHT_DECAY * w), m_new

    stores = []
    for i, (m, r0, n) in enumerate(PIECES):
        scale = inv[:, m:m + 1]
        buf, c0 = held[m]

        for k in range(n // GROUP):
            rows = pl.ds(r0 + GROUP * k, GROUP)
            u = buf[rows, pl.ds(c0 // LANE * LANE, c0 % LANE + HELD[1][m])][:, c0 % LANE:]
            w_new, m_new = finish(u * scale, w_in[m][rows, :], m_in[m][rows, :])
            w_buf[m][rows, :] = w_new
            m_buf[m][rows, :] = m_new
        rows = pl.ds(r0, n)
        for j, (src, dst) in enumerate(((w_buf, w_out), (m_buf, m_out))):
            stores.append(pltpu.make_async_copy(src[m].at[rows, :], dst[m].at[rows, :], out_sem.at[i, j]))
            stores[-1].start()
    w_new, m_new = finish(hv[...] * inv[:, VEC_AT:VEC_AT + 1], wv[...], mv[...])
    wv_out[...] = w_new
    mv_out[...] = m_new
    for src, dst in ((vrq, vrq_out), (vro, vro_out), (vru, vru_out), (vrd, vrd_out),
                     (vcq, vcq_out), (vco, vco_out), (vcu, vcu_out), (vcd, vcd_out), (vv, vv_out)):
        dst[...] = src[...]
    for copy in stores:
        copy.wait()


IN_HBM = pl.BlockSpec(memory_space=pltpu.HBM)
IN_VMEM = pl.BlockSpec(memory_space=pltpu.VMEM)
MIB = 1024 * 1024


def f32(*shape):
    return jax.ShapeDtypeStruct(shape, F32)


def vmem(*shape):
    return pltpu.VMEM(shape, F32)


def local_step(g_qkv, g_out, g_up, g_down, g_vec, w_qkv, w_out, w_up, w_down, w_vec,
               m_qkv, m_out, m_up, m_down, m_vec, vr_qkv, vc_qkv, vr_out, vc_out,
               vr_up, vc_up, vr_down, vc_down, v_vec):
    dma = pltpu.SemaphoreType.DMA
    rows_shapes = [(1, n) for n in ROWS]
    cols_shapes = [(1, n) for n in COLS]
    h_shapes = [(R, QO), (R, UP), (DC, DR)]
    wide_u, wide_d, vec = (R, UP), (DC, DR), (1, VEC)
    shapes = [
        (SLOTS, LANE, QO), (2, 2) + wide_u, (2, 2) + wide_d,
        (STEPS, LANE, QO), (2, 2) + wide_u, (2, 2) + wide_d, (STEPS, 2, 2, R, LANE),
        (STEPS, 2, R, LANE), (2,) + wide_u, (2,) + wide_d, (STEPS, R, LANE), wide_u, wide_d,
        vec, (3,) + vec, (2,) + vec, vec] + rows_shapes + cols_shapes + [
        (R, LANE), (R, LANE), (STEPS, SUB, LANE), (SUB, UP), (SUB, DR)] + [(SUB, LANE)] * 4 + [
        (1, WIDE), (1, DR),
        (FSDP, 1, WIDE), (TP, SUB, LANE), (TP, 1, DR), (FSDP, SUB, LANE),
        (DEVICES, 1, LANE), (DEVICES, 1, LANE)]
    sems = [(3, 2, STEPS)] * 2 + [(3,), (3, 2), (3, 2)] + [(3, 2, STEPS)] * 2 + [(1,), (3,), (3,), (9,), (6,), (6,)]
    inputs = [pltpu.with_memory_space_constraint(a, pltpu.HBM)
              for a in (g_qkv[0, 0].T, g_out[0, 0].T, g_up.reshape(2, 2, 2, R, UP), g_down[0, 0].T, g_vec[0],
                        vr_qkv, vr_out, vr_up, vr_down, vc_qkv, vc_out, vc_up, vc_down, v_vec)]
    reduced = pl.pallas_call(
        reduce_kernel,
        name="reduce_and_scale",
        out_shape=[f32(*s) for s in h_shapes + [vec, (1, LANE)] + rows_shapes + cols_shapes + [vec]],
        in_specs=[IN_HBM] * 14,
        out_specs=[IN_VMEM] * 14,
        scratch_shapes=[vmem(*s) for s in shapes] + [dma(s) for s in sems],
        compiler_params=pltpu.CompilerParams(
            collective_id=0, has_side_effects=True, vmem_limit_bytes=A_MIB * MIB),
    )(*inputs)

    ws = [w_qkv[0], w_out[0], w_up[0], w_down[0].T, w_vec]
    ms = [m_qkv[0], m_out[0], m_up[0], m_down[0].T, m_vec]
    mats = list(zip(*HELD))
    outs = pl.pallas_call(
        update_kernel,
        name="update",
        out_shape=([f32(*s) for s in mats + [vec]] + [jax.ShapeDtypeStruct(s, BF16) for s in mats + [vec]]
                   + [f32(*s) for m in range(4) for s in (rows_shapes[m], cols_shapes[m])] + [f32(*vec)]),
        in_specs=[IN_VMEM] * 24,
        out_specs=([IN_HBM] * 4 + [IN_VMEM]) * 2 + [IN_VMEM] * 9,
        scratch_shapes=([vmem(*s) for s in mats] + [pltpu.VMEM(s, BF16) for s in mats] + [dma((len(PIECES), 2))]),
        compiler_params=pltpu.CompilerParams(vmem_limit_bytes=B_MIB * MIB),
    )(*reduced, *ws, *ms)
    outs = list(outs)
    for i in range(10):
        if i % 5 == 3:
            outs[i] = outs[i].T
        if i % 5 != 4:
            outs[i] = outs[i][None]
    return tuple(outs)


A_MIB, B_MIB = 46, 12


def solution(mesh):
    grad_spec = P("fsdp", None, None, "tp")
    vec_grad_spec = P("fsdp", None, "tp")
    mat_spec = P(None, "fsdp", "tp")
    vec_spec = P(None, "tp")
    row_spec = P(None, "fsdp")
    col_spec = P(None, "tp")
    state_specs = ((mat_spec,) * 4 + (vec_spec,) + (mat_spec,) * 4 + (vec_spec,)
                   + (row_spec, col_spec) * 4 + (vec_spec,))
    arg_specs = (grad_spec,) * 4 + (vec_grad_spec,) + state_specs
    return jax.shard_map(local_step, mesh=mesh, in_specs=arg_specs, out_specs=state_specs, check_vma=False)
```

time: 432 us -> 132 us (0.31)
  waiting for transfers between devices: 220 us -> 0 us
  blocking collectives: 149 us -> 0 us
  Pallas kernels: 0 us -> 131 us
  other arithmetic: 27 us -> 0 us
  between operations: 24 us -> 0.83 us
  local copies, waits for them, and re-layouts: 10.8 us -> 0.04 us
    reduce_scatter x4 -> x0, waiting for transfers between devices: 219 us -> none  [local_step(): lax.psum_scatter(g_part[0], 'fsdp', scatter_dimension=1, tiled=True)]
    psum x6 -> x0, blocking collectives: 149 us -> none  [the longest x1 37.7 us: matrix_step(): lax.psum(jnp.sum(jnp.square(update_val), axis=(1, 2)), ('tp', 'fsdp'))]
    pallas_call x0 -> x2, Pallas kernels: none -> 131 us  [the longest x1 127 us: local_step(): pl.pallas_call(reduce_kernel, name='reduce_and_scale', out_shape=[f32(*s)...]
    reduce_sum x18 -> x0, other arithmetic: 17.2 us -> none  [the longest x4 8.01 us: local_step(): mat_sq = sum([jnp.sum(jnp.square(g_shard)) for g_shard in grad_shards])]
    unnamed x54 -> x20, local copies, waits for them, and re-layouts: 10.8 us -> 0.04 us
    sub x5 -> x0, other arithmetic: 8.01 us -> none  [finish_step(): weight - LEARN_RATE * (moment_new.astype(jnp.float32) + WEIGHT_DECAY * we...]
  transfers between devices with their start and end apart: 4 -> 0, of which waited for: 4 -> 0; matrix products, arithmetic and copies ran while one was open for 3% -> 0% of each run, Pallas kernels for 0% -> 0%
where the time goes in v1:
time: 132 us; the launch traced here: 131 us
  Pallas kernels  131 us (99%)
    pallas_call x1, Pallas kernels, local_step(): pl.pallas_call(reduce_kernel, name='reduce_and_scale', out_shape=[f32(*s)...  127 us
    pallas_call x1, Pallas kernels, local_step(): pl.pallas_call(update_kernel, name='update', out_shape=[f32(*s) for s in...  3.5 us

profile of v1, /device:TPU:0, one launch (start us, length us, event | category | flops | bytes accessed | tf_op | source)
XLA Modules:
  0.0 131.4 jit_solution(853395661625356610)
XLA Ops:
  0.7 0.0 copy-start
  0.7 0.0 copy-start.1
  0.7 0.0 copy-start.2
  0.7 0.0 copy-start.3
  0.7 0.0 copy-start.4
  0.7 0.0 copy-start.5
  0.7 0.0 copy-start.6
  0.7 0.0 copy-start.7
  0.7 0.0 copy-start.8
  0.8 0.0 copy-start.9
  0.8 127.0 %reduce_and_scale.1 = (f32[176,1408]{1,0:T(8,128)S(1)}, f32[176,1536]{1,0:T(8,128)S(1)}, f32[352,768]{1,0:T(8,128)S(1)}, f32[1,4704]{1,0:T(1,128)S(1)}, f32[1,12...) custom-call(f32[1056,1408]{1,0:T(8,128)} %bitcast.45, ...), custom_call_target="tpu_custom_call" | custom-call | tf_op jit(solution)/shard_map/reduce_and_scale/pallas_call | solution.py:571
  127.8 0.0 copy-done
  127.8 0.0 copy-done.1
  127.8 0.0 copy-done.2
  127.8 0.0 copy-done.3
  127.8 0.0 copy-done.4
  127.9 0.0 copy-done.5
  127.9 0.0 copy-done.6
  127.9 0.0 copy-done.7
  127.9 0.0 copy-done.8
  127.9 0.0 copy-done.9
  127.9 3.5 %update.1 = (f32[176,1056]{1,0:T(8,128)}, f32[176,352]{1,0:T(8,128)}, f32[176,1536]{1,0:T(8,128)}, f32[352,768]{1,0:T(8,128)}, f32[1,4704]{1,0:T(1,128)}, /*inde...) custom-call(f32[176,1408]{1,0:T(8,128)S(1)} %get-tuple-element.52.re, ...), custom_call_target="tpu_custom_call" | custom-call | tf_op jit(solution)/shard_map/update/pallas_call | solution.py:585
Async XLA Ops:
  0.7 127.1 %copy-start = (f32[1,176,1536]{2,1,0:T(8,128)S(1)}, f32[1,176,1536]{2,1,0:T(8,128)}, u32[]{:S(2)}) copy-start(f32[1,176,1536]{2,1,0:T(8,128)} %param.31) | copy-start | bytes 3244036
  0.7 127.1 %copy-start.1 = (f32[1,768,352]{1,2,0:T(8,128)S(1)}, f32[1,768,352]{1,2,0:T(8,128)}, u32[]{:S(2)}) copy-start(f32[1,768,352]{1,2,0:T(8,128)} %param.32) | copy-start | bytes 3244036
  0.7 127.1 %copy-start.2 = (f32[1,176,1056]{2,1,0:T(8,128)S(1)}, f32[1,176,1056]{2,1,0:T(8,128)}, u32[]{:S(2)}) copy-start(f32[1,176,1056]{2,1,0:T(8,128)} %param.29) | copy-start | bytes 2230276
  0.7 127.1 %copy-start.3 = (bf16[1,176,1536]{2,1,0:T(8,128)(2,1)S(1)}, bf16[1,176,1536]{2,1,0:T(8,128)(2,1)}, u32[]{:S(2)}) copy-start(bf16[1,176,1536]{2,1,0:T(8,128)(2,1)} %param.36) | copy-start | bytes 1622020
  0.7 127.1 %copy-start.4 = (bf16[1,768,352]{1,2,0:T(8,128)(2,1)S(1)}, bf16[1,768,352]{1,2,0:T(8,128)(2,1)}, u32[]{:S(2)}) copy-start(bf16[1,768,352]{1,2,0:T(8,128)(2,1)} %param.37) | copy-start | bytes 1622020
  0.7 127.1 %copy-start.5 = (bf16[1,176,1056]{2,1,0:T(8,128)(2,1)S(1)}, bf16[1,176,1056]{2,1,0:T(8,128)(2,1)}, u32[]{:S(2)}) copy-start(bf16[1,176,1056]{2,1,0:T(8,128)(2,1)} %param.34) | copy-start | bytes 1115140
  0.7 127.1 %copy-start.6 = (f32[1,176,352]{2,1,0:T(8,128)S(1)}, f32[1,176,352]{2,1,0:T(8,128)}, u32[]{:S(2)}) copy-start(f32[1,176,352]{2,1,0:T(8,128)} %param.30) | copy-start | bytes 743428
  0.7 127.1 %copy-start.7 = (bf16[1,176,352]{2,1,0:T(8,128)(2,1)S(1)}, bf16[1,176,352]{2,1,0:T(8,128)(2,1)}, u32[]{:S(2)}) copy-start(bf16[1,176,352]{2,1,0:T(8,128)(2,1)} %param.35) | copy-start | bytes 371716
  0.7 127.1 %copy-start.8 = (f32[1,4704]{1,0:T(1,128)S(1)}, f32[1,4704]{1,0:T(1,128)}, u32[]{:S(2)}) copy-start(f32[1,4704]{1,0:T(1,128)} %refs_18_.1) | copy-start | bytes 56452
  0.8 127.1 %copy-start.9 = (bf16[1,4704]{1,0:T(2,128)(2,1)S(1)}, bf16[1,4704]{1,0:T(2,128)(2,1)}, u32[]{:S(2)}) copy-start(bf16[1,4704]{1,0:T(2,128)(2,1)} %refs_23_.1) | copy-start | bytes 28228

commit v2 on v1

--- a/solution.py
+++ b/solution.py
@@ -87,7 +87,7 @@
      p_q, p_o, cs_qo, cs_u, rs_d, rp_acc, rpd_acc, rp_old, rpd_old, col_buf, rowd_buf,
      cs_all, rp_all, rsd_all, rpd_all, s_all, u_all,
      own_sem, peer_sem, push_sem, first_sem, second_sem, a_sem, b_sem,
-     vec_sem, vec_send, vec_recv, small_sem, stat_send, stat_recv) = refs
+     vec_sem, vec_send, vec_recv, small_sem, stat_send, stat_recv, round_sem) = refs
 
     me = lax.axis_index("fsdp")
     z = lax.axis_index("tp")
@@ -99,6 +99,16 @@
     across_x = {"fsdp": me + 2 - 4 * x}
     across_y = {"fsdp": me + 4 - 8 * y}
     every = slice(None)
+
+    def flip(v, bits):
+        for bit in range(3):
+            step = 2 ** bit
+            if bits & step:
+                v = v + step - 2 * step * lax.rem(v // step, 2)
+        return v
+
+    others = [{"tp": flip(z, a), "fsdp": flip(me, b)} for a in range(TP - 1, -1, -1)
+              for b in range(FSDP - 1, -1, -1) if a + b > 0]
 
     owns, peers = (own_u, own_qo, own_d), (peer_u, peer_qo, peer_d)
     sums, firsts, seconds = (own_u, s_qo, own_d), (a_u, a_qo, a_d), (b_u, b_qo, b_d)
@@ -191,13 +201,19 @@
         copy.start()
     barrier = pltpu.get_barrier_semaphore()
 
-    def other(d):
-        to = lax.rem(linear + d, DEVICES)
-        return {"tp": to // FSDP, "fsdp": lax.rem(to, FSDP)}
-
-    for d in range(1, DEVICES):
-        pl.semaphore_signal(barrier, inc=1, device_id=other(d), device_id_type=MESH)
-    pl.semaphore_wait(barrier, DEVICES - 1)
+    def signal(sem, to):
+        pl.semaphore_signal(sem, inc=1, device_id=to, device_id_type=MESH)
+
+    def signal_z(sem):
+        pl.when(z > 0)(lambda: signal(sem, {"tp": z - 1}))
+        pl.when(z < TP - 1)(lambda: signal(sem, {"tp": z + 1}))
+
+    beside = jnp.where(z > 0, 1, 0) + jnp.where(z < TP - 1, 1, 0)
+    near = (mate, across_x, across_y)
+    for to in near:
+        signal(barrier, to)
+    signal_z(barrier)
+    pl.semaphore_wait(barrier, len(near) + beside)
 
     for step in range(LOOK):
         start_kind(U_, step, True)
@@ -258,6 +274,13 @@
     masks = [jnp.logical_and(lane >= ROW_TILES * m, lane < ROW_TILES * (m + 1)) for m in range(3)]
     old_sums = [total(jnp.where(masks[m], old, 0.0)) for m in range(3)] + [total(r_d[...])]
 
+    for i, to in enumerate(near):
+        signal(round_sem.at[i], to)
+        pl.semaphore_wait(round_sem.at[i], 1)
+    for i in range(len(near), len(near) + TP - 2):
+        signal_z(round_sem.at[i])
+        pl.semaphore_wait(round_sem.at[i], beside)
+
     def stage2(kind):
         def body(k, _):
             for side in range(2):
@@ -328,8 +351,8 @@
                  {axis: lax.rem(here + d, n)}).start()
 
     def to_all(buf, i):
-        for d in range(1, DEVICES):
-            send(buf.at[linear], buf.at[linear], stat_send.at[i], stat_recv.at[i], other(d)).start()
+        for to in others:
+            send(buf.at[linear], buf.at[linear], stat_send.at[i], stat_recv.at[i], to).start()
 
     def spread(buf, i, n):
         part = buf.at[pl.ds(0, n - 1)]
@@ -499,7 +522,7 @@
      wq, wo, wu, wd, wv, mq, mo, mu, md, mv,
      wq_out, wo_out, wu_out, wd_out, wv_out, mq_out, mo_out, mu_out, md_out, mv_out,
      vrq_out, vcq_out, vro_out, vco_out, vru_out, vcu_out, vrd_out, vcd_out, vv_out,
-     bwq, bwo, bwu, bwd, bmq, bmo, bmu, bmd, out_sem) = refs
+     bwq, bwo, bwu, bwd, bmq, bmo, bmu, bmd, bwv, bmv, out_sem, small_sem) = refs
     held = ((hqo, 0), (hqo, COLS[0]), (hu, 0), (hd, 0))
     w_in, m_in = (wq, wo, wu, wd), (mq, mo, mu, md)
     w_buf, m_buf = (bwq, bwo, bwu, bwd), (bmq, bmo, bmu, bmd)
@@ -509,7 +532,16 @@
         m_new = (MOMENTUM * m.astype(F32) + (1.0 - MOMENTUM) * u).astype(BF16)
         return w - LEARN_RATE * (m_new.astype(F32) + WEIGHT_DECAY * w), m_new
 
-    stores = []
+    passed = ((vrq, vrq_out), (vro, vro_out), (vru, vru_out), (vrd, vrd_out),
+              (vcq, vcq_out), (vco, vco_out), (vcu, vcu_out), (vcd, vcd_out), (vv, vv_out))
+    stores = [pltpu.make_async_copy(src, dst, small_sem.at[i]) for i, (src, dst) in enumerate(passed)]
+    w_new, m_new = finish(hv[...] * inv[:, VEC_AT:VEC_AT + 1], wv[...], mv[...])
+    bwv[...] = w_new
+    bmv[...] = m_new
+    stores.append(pltpu.make_async_copy(bwv, wv_out, small_sem.at[len(passed)]))
+    stores.append(pltpu.make_async_copy(bmv, mv_out, small_sem.at[len(passed) + 1]))
+    for copy in stores:
+        copy.start()
     for i, (m, r0, n) in enumerate(PIECES):
         scale = inv[:, m:m + 1]
         buf, c0 = held[m]
@@ -524,12 +556,6 @@
         for j, (src, dst) in enumerate(((w_buf, w_out), (m_buf, m_out))):
             stores.append(pltpu.make_async_copy(src[m].at[rows, :], dst[m].at[rows, :], out_sem.at[i, j]))
             stores[-1].start()
-    w_new, m_new = finish(hv[...] * inv[:, VEC_AT:VEC_AT + 1], wv[...], mv[...])
-    wv_out[...] = w_new
-    mv_out[...] = m_new
-    for src, dst in ((vrq, vrq_out), (vro, vro_out), (vru, vru_out), (vrd, vrd_out),
-                     (vcq, vcq_out), (vco, vco_out), (vcu, vcu_out), (vcd, vcd_out), (vv, vv_out)):
-        dst[...] = src[...]
     for copy in stores:
         copy.wait()
 
@@ -574,7 +600,7 @@
         out_shape=[f32(*s) for s in h_shapes + [vec, (1, LANE)] + rows_shapes + cols_shapes + [vec]],
         in_specs=[IN_HBM] * 14,
         out_specs=[IN_VMEM] * 14,
-        scratch_shapes=[vmem(*s) for s in shapes] + [dma(s) for s in sems],
+        scratch_shapes=[vmem(*s) for s in shapes] + [dma(s) for s in sems] + [pltpu.SemaphoreType.REGULAR((TP + 1,))],
         compiler_params=pltpu.CompilerParams(
             collective_id=0, has_side_effects=True, vmem_limit_bytes=A_MIB * MIB),
     )(*inputs)
@@ -588,8 +614,9 @@
         out_shape=([f32(*s) for s in mats + [vec]] + [jax.ShapeDtypeStruct(s, BF16) for s in mats + [vec]]
                    + [f32(*s) for m in range(4) for s in (rows_shapes[m], cols_shapes[m])] + [f32(*vec)]),
         in_specs=[IN_VMEM] * 24,
-        out_specs=([IN_HBM] * 4 + [IN_VMEM]) * 2 + [IN_VMEM] * 9,
-        scratch_shapes=([vmem(*s) for s in mats] + [pltpu.VMEM(s, BF16) for s in mats] + [dma((len(PIECES), 2))]),
+        out_specs=[IN_HBM] * 19,
+        scratch_shapes=([vmem(*s) for s in mats] + [pltpu.VMEM(s, BF16) for s in mats]
+                        + [vmem(*vec), pltpu.VMEM(vec, BF16), dma((len(PIECES), 2)), dma((11,))]),
         compiler_params=pltpu.CompilerParams(vmem_limit_bytes=B_MIB * MIB),
     )(*reduced, *ws, *ms)
     outs = list(outs)

time: 132 us -> 128 us (0.970)
  Pallas kernels: 131 us -> 127 us
    pallas_call x1, Pallas kernels: 127 us -> 124 us  [local_step(): pl.pallas_call(reduce_kernel, name='reduce_and_scale', out_shape=[f32(*s)...]
where the time goes in v2:
time: 128 us
  Pallas kernels  127 us (99%)
    pallas_call x1, Pallas kernels, local_step(): pl.pallas_call(reduce_kernel, name='reduce_and_scale', out_shape=[f32(*s)...  124 us
    pallas_call x1, Pallas kernels, local_step(): pl.pallas_call(update_kernel, name='update', out_shape=[f32(*s) for s in...  2.99 us

profile of v2, /device:TPU:0, one launch (start us, length us, event | category | flops | bytes accessed | tf_op | source)
XLA Modules:
  0.0 127.6 jit_solution(10231063404423550928)
XLA Ops:
  0.7 0.0 copy-start
  0.7 0.0 copy-start.1
  0.7 0.0 copy-start.2
  0.7 0.0 copy-start.3
  0.7 0.0 copy-start.4
  0.7 0.0 copy-start.5
  0.7 0.0 copy-start.6
  0.7 0.0 copy-start.7
  0.7 0.0 copy-start.8
  0.8 0.0 copy-start.9
  0.8 123.7 %reduce_and_scale.1 = (f32[176,1408]{1,0:T(8,128)S(1)}, f32[176,1536]{1,0:T(8,128)S(1)}, f32[352,768]{1,0:T(8,128)S(1)}, f32[1,4704]{1,0:T(1,128)S(1)}, f32[1,12...) custom-call(f32[1056,1408]{1,0:T(8,128)} %bitcast.45, ...), custom_call_target="tpu_custom_call" | custom-call | tf_op jit(solution)/shard_map/reduce_and_scale/pallas_call | solution.py:597
  124.5 0.0 copy-done
  124.5 0.0 copy-done.1
  124.5 0.0 copy-done.2
  124.5 0.0 copy-done.3
  124.5 0.0 copy-done.4
  124.5 0.0 copy-done.5
  124.5 0.0 copy-done.6
  124.5 0.0 copy-done.7
  124.6 0.0 copy-done.8
  124.6 0.0 copy-done.9
  124.6 3.0 %update.1 = (f32[176,1056]{1,0:T(8,128)}, f32[176,352]{1,0:T(8,128)}, f32[176,1536]{1,0:T(8,128)}, f32[352,768]{1,0:T(8,128)}, f32[1,4704]{1,0:T(1,128)}, /*inde...) custom-call(f32[176,1408]{1,0:T(8,128)S(1)} %get-tuple-element.52.re, ...), custom_call_target="tpu_custom_call" | custom-call | tf_op jit(solution)/shard_map/update/pallas_call | solution.py:611
Async XLA Ops:
  0.7 123.8 %copy-start = (f32[1,176,1536]{2,1,0:T(8,128)S(1)}, f32[1,176,1536]{2,1,0:T(8,128)}, u32[]{:S(2)}) copy-start(f32[1,176,1536]{2,1,0:T(8,128)} %param.31) | copy-start | bytes 3244036
  0.7 123.8 %copy-start.1 = (f32[1,768,352]{1,2,0:T(8,128)S(1)}, f32[1,768,352]{1,2,0:T(8,128)}, u32[]{:S(2)}) copy-start(f32[1,768,352]{1,2,0:T(8,128)} %param.32) | copy-start | bytes 3244036
  0.7 123.8 %copy-start.2 = (f32[1,176,1056]{2,1,0:T(8,128)S(1)}, f32[1,176,1056]{2,1,0:T(8,128)}, u32[]{:S(2)}) copy-start(f32[1,176,1056]{2,1,0:T(8,128)} %param.29) | copy-start | bytes 2230276
  0.7 123.8 %copy-start.3 = (bf16[1,176,1536]{2,1,0:T(8,128)(2,1)S(1)}, bf16[1,176,1536]{2,1,0:T(8,128)(2,1)}, u32[]{:S(2)}) copy-start(bf16[1,176,1536]{2,1,0:T(8,128)(2,1)} %param.36) | copy-start | bytes 1622020
  0.7 123.8 %copy-start.4 = (bf16[1,768,352]{1,2,0:T(8,128)(2,1)S(1)}, bf16[1,768,352]{1,2,0:T(8,128)(2,1)}, u32[]{:S(2)}) copy-start(bf16[1,768,352]{1,2,0:T(8,128)(2,1)} %param.37) | copy-start | bytes 1622020
  0.7 123.8 %copy-start.5 = (bf16[1,176,1056]{2,1,0:T(8,128)(2,1)S(1)}, bf16[1,176,1056]{2,1,0:T(8,128)(2,1)}, u32[]{:S(2)}) copy-start(bf16[1,176,1056]{2,1,0:T(8,128)(2,1)} %param.34) | copy-start | bytes 1115140
  0.7 123.8 %copy-start.6 = (f32[1,176,352]{2,1,0:T(8,128)S(1)}, f32[1,176,352]{2,1,0:T(8,128)}, u32[]{:S(2)}) copy-start(f32[1,176,352]{2,1,0:T(8,128)} %param.30) | copy-start | bytes 743428
  0.7 123.8 %copy-start.7 = (bf16[1,176,352]{2,1,0:T(8,128)(2,1)S(1)}, bf16[1,176,352]{2,1,0:T(8,128)(2,1)}, u32[]{:S(2)}) copy-start(bf16[1,176,352]{2,1,0:T(8,128)(2,1)} %param.35) | copy-start | bytes 371716
  0.7 123.8 %copy-start.8 = (f32[1,4704]{1,0:T(1,128)S(1)}, f32[1,4704]{1,0:T(1,128)}, u32[]{:S(2)}) copy-start(f32[1,4704]{1,0:T(1,128)} %refs_18_.1) | copy-start | bytes 56452
  0.8 123.8 %copy-start.9 = (bf16[1,4704]{1,0:T(2,128)(2,1)S(1)}, bf16[1,4704]{1,0:T(2,128)(2,1)}, u32[]{:S(2)}) copy-start(bf16[1,4704]{1,0:T(2,128)(2,1)} %refs_23_.1) | copy-start | bytes 28228

commit v3 on v2

--- a/solution.py
+++ b/solution.py
@@ -33,6 +33,7 @@
 D_TILES = DC // SUB
 WIDE = -(-(QO + UP) // (SUB * LANE)) * SUB * LANE
 LOOK, SLOTS = 3, 4
+OPENING = ((1,), (2, 3))
 U_, QO_, D_ = 0, 1, 2
 VR_AT, VEC_AT = 4, 8
 
@@ -80,14 +81,14 @@
     (gq, go, gu, gd, gv, vrq, vro, vru, vrd, vcq, vco, vcu, vcd, vv,
      hqo, hu, hd, hv, inv_out,
      n_rq, n_ro, n_ru, n_rd, n_cq, n_co, n_cu, n_cd, vv_new,
-     own_qo, own_u, own_d, peer_qo, peer_u, peer_d, s_qo,
+     stage, own_qo, own_u, own_d, peer_qo, peer_u, peer_d, s_qo,
      a_qo, a_u, a_d, b_qo, b_u, b_d,
      vec_own, vec_in, vec_mid, vv_in,
      r_q, r_o, r_u, r_d, c_q, c_o, c_u, c_d,
      p_q, p_o, cs_qo, cs_u, rs_d, rp_acc, rpd_acc, rp_old, rpd_old, col_buf, rowd_buf,
      cs_all, rp_all, rsd_all, rpd_all, s_all, u_all,
      own_sem, peer_sem, push_sem, first_sem, second_sem, a_sem, b_sem,
-     vec_sem, vec_send, vec_recv, small_sem, stat_send, stat_recv, round_sem) = refs
+     vec_sem, vec_send, vec_recv, small_sem, stat_send, stat_recv, stage_sem, round_sem) = refs
 
     me = lax.axis_index("fsdp")
     z = lax.axis_index("tp")
@@ -194,11 +195,11 @@
     small_copies = [pltpu.make_async_copy(a, b, small_sem.at[i]) for i, (a, b) in enumerate(smalls)]
     vec_copy = pltpu.make_async_copy(gv, vec_own, vec_sem.at[0])
 
-    for step in range(LOOK):
-        start_kind(U_, step, False)
-    vec_copy.start()
-    for copy in small_copies:
+    staged = [pltpu.make_async_copy(gu.at[(every, every, 1 - core) + index(U_, (), side, 0)],
+                                    stage.at[side], stage_sem.at[side]) for side in range(2)]
+    for copy in staged:
         copy.start()
+    start_kind(U_, 0, False)
     barrier = pltpu.get_barrier_semaphore()
 
     def signal(sem, to):
@@ -215,13 +216,16 @@
     signal_z(barrier)
     pl.semaphore_wait(barrier, len(near) + beside)
 
-    for step in range(LOOK):
-        start_kind(U_, step, True)
-    vec_copy.wait()
+    for side in range(2):
+        staged[side].wait()
+        send(stage.at[side], peer_u.at[index(U_, (every, every), side, 0)],
+             push_sem.at[U_], peer_sem.at[U_, side, 0], mate).start()
+    vec_copy.start()
+    for copy in small_copies:
+        copy.start()
     vec_core = send(vec_own, vec_in.at[0], vec_send.at[0], vec_recv.at[0], mate)
     vec_x = send(vec_mid.at[0], vec_in.at[1], vec_send.at[1], vec_recv.at[1], across_x)
     vec_y = send(vec_mid.at[1], vec_in.at[2], vec_send.at[2], vec_recv.at[2], across_y)
-    vec_core.start()
 
     def turn(k, which):
         slot = lax.rem(k, SLOTS)
@@ -236,10 +240,11 @@
                     first_row = start - R * (2 * b + which)
                     s_qo[k, b // 2, b % 2, pl.ds(first_row, stop - start), :] = turned[start - lo:stop - lo]
 
-    def stage1(kind):
+    def stage1(kind, opening=False):
         def body(k, _):
-            start_loads(k + kind * STEPS + LOOK, False)
-            start_loads(k + kind * STEPS + LOOK, True)
+            if not opening:
+                start_loads(k + kind * STEPS + LOOK, False)
+                start_loads(k + kind * STEPS + LOOK, True)
             if kind == QO_:
                 loaded(kind, 0, k)
                 for which in range(2):
@@ -251,14 +256,20 @@
                         at = index(kind, (b // 2, b % 2), side, k)
                         owns[kind][at] = owns[kind][at] + peers[kind][at]
                 first(kind, side, chunk(k), a_sem.at[kind, side, k]).start()
+                if opening:
+                    for step in OPENING[side]:
+                        start_kind(U_, step, False)
+                        start_kind(U_, step, True)
             return _
         return body
 
+    stage1(U_, True)(0, 0)
+    vec_copy.wait()
+    vec_core.start()
+    lax.fori_loop(1, STEPS, stage1(U_), 0)
     vec_core.wait_recv()
     vec_mid[0] = vec_own[...] + vec_in[0]
-    lax.fori_loop(0, 1, stage1(U_), 0)
     vec_x.start()
-    lax.fori_loop(1, STEPS, stage1(U_), 0)
     for kind in (QO_, D_):
         lax.fori_loop(0, STEPS, stage1(kind), 0)
 
@@ -512,7 +523,7 @@
     spread(u_all, len(groups) - 1, DEVICES).wait_send()
 
 
-PIECES = ((3, 0, HALF_DC), (3, HALF_DC, HALF_DC), (2, 0, R), (0, 0, R), (1, 0, R))
+PIECES = ((3, 0, 48), (3, 48, 128), (3, 176, 176), (2, 0, 96), (2, 96, 80), (0, 0, 96), (0, 96, 80), (1, 0, R))
 HELD = (ROWS[:3] + (DC,), COLS[:3] + (DR,))
 GROUP = 16
 
@@ -582,7 +593,7 @@
     h_shapes = [(R, QO), (R, UP), (DC, DR)]
     wide_u, wide_d, vec = (R, UP), (DC, DR), (1, VEC)
     shapes = [
-        (SLOTS, LANE, QO), (2, 2) + wide_u, (2, 2) + wide_d,
+        (2, 2, 2, SUB, UP), (SLOTS, LANE, QO), (2, 2) + wide_u, (2, 2) + wide_d,
         (STEPS, LANE, QO), (2, 2) + wide_u, (2, 2) + wide_d, (STEPS, 2, 2, R, LANE),
         (STEPS, 2, R, LANE), (2,) + wide_u, (2,) + wide_d, (STEPS, R, LANE), wide_u, wide_d,
         vec, (3,) + vec, (2,) + vec, vec] + rows_shapes + cols_shapes + [
@@ -590,7 +601,7 @@
         (1, WIDE), (1, DR),
         (FSDP, 1, WIDE), (TP, SUB, LANE), (TP, 1, DR), (FSDP, SUB, LANE),
         (DEVICES, 1, LANE), (DEVICES, 1, LANE)]
-    sems = [(3, 2, STEPS)] * 2 + [(3,), (3, 2), (3, 2)] + [(3, 2, STEPS)] * 2 + [(1,), (3,), (3,), (9,), (6,), (6,)]
+    sems = [(3, 2, STEPS)] * 2 + [(3,), (3, 2), (3, 2)] + [(3, 2, STEPS)] * 2 + [(1,), (3,), (3,), (9,), (6,), (6,), (2,)]
     inputs = [pltpu.with_memory_space_constraint(a, pltpu.HBM)
               for a in (g_qkv[0, 0].T, g_out[0, 0].T, g_up.reshape(2, 2, 2, R, UP), g_down[0, 0].T, g_vec[0],
                         vr_qkv, vr_out, vr_up, vr_down, vc_qkv, vc_out, vc_up, vc_down, v_vec)]

time: 128 us -> 126 us (0.984)
  Pallas kernels: 127 us -> 125 us
    pallas_call x1, Pallas kernels: 124 us -> 122 us  [local_step(): pl.pallas_call(reduce_kernel, name='reduce_and_scale', out_shape=[f32(*s)...]
where the time goes in v3:
time: 126 us
  Pallas kernels  125 us (99%)
    pallas_call x1, Pallas kernels, local_step(): pl.pallas_call(reduce_kernel, name='reduce_and_scale', out_shape=[f32(*s)...  122 us
    pallas_call x1, Pallas kernels, local_step(): pl.pallas_call(update_kernel, name='update', out_shape=[f32(*s) for s in...  2.77 us

profile of v3, /device:TPU:0, one launch (start us, length us, event | category | flops | bytes accessed | tf_op | source)
XLA Modules:
  0.0 125.9 jit_solution(9291806851498964980)
XLA Ops:
  0.7 0.0 copy-start
  0.7 0.0 copy-start.1
  0.7 0.0 copy-start.2
  0.7 0.0 copy-start.3
  0.7 0.0 copy-start.4
  0.7 0.0 copy-start.5
  0.7 0.0 copy-start.6
  0.7 0.0 copy-start.7
  0.7 0.0 copy-start.8
  0.8 0.0 copy-start.9
  0.8 122.3 %reduce_and_scale.1 = (f32[176,1408]{1,0:T(8,128)S(1)}, f32[176,1536]{1,0:T(8,128)S(1)}, f32[352,768]{1,0:T(8,128)S(1)}, f32[1,4704]{1,0:T(1,128)S(1)}, f32[1,12...) custom-call(f32[1056,1408]{1,0:T(8,128)} %bitcast.45, ...), custom_call_target="tpu_custom_call" | custom-call | tf_op jit(solution)/shard_map/reduce_and_scale/pallas_call | solution.py:608
  123.0 0.0 copy-done
  123.0 0.0 copy-done.1
  123.1 0.0 copy-done.2
  123.1 0.0 copy-done.3
  123.1 0.0 copy-done.4
  123.1 0.0 copy-done.5
  123.1 0.0 copy-done.6
  123.1 0.0 copy-done.7
  123.1 0.0 copy-done.8
  123.1 0.0 copy-done.9
  123.1 2.8 %update.1 = (f32[176,1056]{1,0:T(8,128)}, f32[176,352]{1,0:T(8,128)}, f32[176,1536]{1,0:T(8,128)}, f32[352,768]{1,0:T(8,128)}, f32[1,4704]{1,0:T(1,128)}, /*inde...) custom-call(f32[176,1408]{1,0:T(8,128)S(1)} %get-tuple-element.52.re, ...), custom_call_target="tpu_custom_call" | custom-call | tf_op jit(solution)/shard_map/update/pallas_call | solution.py:622
Async XLA Ops:
  0.7 122.4 %copy-start = (f32[1,176,1536]{2,1,0:T(8,128)S(1)}, f32[1,176,1536]{2,1,0:T(8,128)}, u32[]{:S(2)}) copy-start(f32[1,176,1536]{2,1,0:T(8,128)} %param.31) | copy-start | bytes 3244036
  0.7 122.4 %copy-start.1 = (f32[1,768,352]{1,2,0:T(8,128)S(1)}, f32[1,768,352]{1,2,0:T(8,128)}, u32[]{:S(2)}) copy-start(f32[1,768,352]{1,2,0:T(8,128)} %param.32) | copy-start | bytes 3244036
  0.7 122.4 %copy-start.2 = (f32[1,176,1056]{2,1,0:T(8,128)S(1)}, f32[1,176,1056]{2,1,0:T(8,128)}, u32[]{:S(2)}) copy-start(f32[1,176,1056]{2,1,0:T(8,128)} %param.29) | copy-start | bytes 2230276
  0.7 122.4 %copy-start.3 = (bf16[1,176,1536]{2,1,0:T(8,128)(2,1)S(1)}, bf16[1,176,1536]{2,1,0:T(8,128)(2,1)}, u32[]{:S(2)}) copy-start(bf16[1,176,1536]{2,1,0:T(8,128)(2,1)} %param.36) | copy-start | bytes 1622020
  0.7 122.4 %copy-start.4 = (bf16[1,768,352]{1,2,0:T(8,128)(2,1)S(1)}, bf16[1,768,352]{1,2,0:T(8,128)(2,1)}, u32[]{:S(2)}) copy-start(bf16[1,768,352]{1,2,0:T(8,128)(2,1)} %param.37) | copy-start | bytes 1622020
  0.7 122.4 %copy-start.5 = (bf16[1,176,1056]{2,1,0:T(8,128)(2,1)S(1)}, bf16[1,176,1056]{2,1,0:T(8,128)(2,1)}, u32[]{:S(2)}) copy-start(bf16[1,176,1056]{2,1,0:T(8,128)(2,1)} %param.34) | copy-start | bytes 1115140
  0.7 122.4 %copy-start.6 = (f32[1,176,352]{2,1,0:T(8,128)S(1)}, f32[1,176,352]{2,1,0:T(8,128)}, u32[]{:S(2)}) copy-start(f32[1,176,352]{2,1,0:T(8,128)} %param.30) | copy-start | bytes 743428
  0.7 122.4 %copy-start.7 = (bf16[1,176,352]{2,1,0:T(8,128)(2,1)S(1)}, bf16[1,176,352]{2,1,0:T(8,128)(2,1)}, u32[]{:S(2)}) copy-start(bf16[1,176,352]{2,1,0:T(8,128)(2,1)} %param.35) | copy-start | bytes 371716
  0.7 122.4 %copy-start.8 = (f32[1,4704]{1,0:T(1,128)S(1)}, f32[1,4704]{1,0:T(1,128)}, u32[]{:S(2)}) copy-start(f32[1,4704]{1,0:T(1,128)} %refs_18_.1) | copy-start | bytes 56452
  0.8 122.4 %copy-start.9 = (bf16[1,4704]{1,0:T(2,128)(2,1)S(1)}, bf16[1,4704]{1,0:T(2,128)(2,1)}, u32[]{:S(2)}) copy-start(bf16[1,4704]{1,0:T(2,128)(2,1)} %refs_23_.1) | copy-start | bytes 28228

commit v4 on v3

--- a/solution.py
+++ b/solution.py
@@ -32,9 +32,13 @@
 ROW_TILES = R // SUB
 D_TILES = DC // SUB
 WIDE = -(-(QO + UP) // (SUB * LANE)) * SUB * LANE
-LOOK, SLOTS = 3, 4
-OPENING = ((1,), (2, 3))
+LOOK, SLOTS = 2, 3
+OPENING = ((1,), (2,))
 U_, QO_, D_ = 0, 1, 2
+BATCH = 6
+BATCHES = ((0, 6), (6, 5))
+SECOND = (BATCHES, BATCHES, ((0, 6), (6, 3), (9, 1), (10, 1)))
+SECOND_AT = (0, 2, 4)
 VR_AT, VEC_AT = 4, 8
 
 
@@ -79,7 +83,9 @@
 
 def reduce_kernel(*refs):
     (gq, go, gu, gd, gv, vrq, vro, vru, vrd, vcq, vco, vcu, vcd, vv,
+     wq, wo, wu, wd, wv, mq, mo, mu, md, mv,
      hqo, hu, hd, hv, inv_out,
+     wq_out, wo_out, wu_out, wd_out, wv_out, mq_out, mo_out, mu_out, md_out, mv_out,
      n_rq, n_ro, n_ru, n_rd, n_cq, n_co, n_cu, n_cd, vv_new,
      stage, own_qo, own_u, own_d, peer_qo, peer_u, peer_d, s_qo,
      a_qo, a_u, a_d, b_qo, b_u, b_d,
@@ -126,31 +132,39 @@
             return lead + (pl.ds(pl.multiple_of(HALF_R * side + SUB * k, SUB), SUB),)
         return lead + (pl.ds(pl.multiple_of(HALF_DC * side + D_STEP * k, SUB), D_STEP),)
 
-    def whole(kind, lead, side):
-        if kind == QO_:
-            return (every,) + lead + (pl.ds(HALF_R * side, HALF_R),)
-        n = HALF_R if kind == U_ else HALF_DC
-        return lead + (pl.ds(n * side, n),)
-
     def first(kind, side, at, sem):
         lead, to = (((every, 1 - x), across_x), ((1 - y, every), across_y))[side]
         return send(sums[kind].at[at(kind, lead, side)], firsts[kind].at[at(kind, (every,), side)],
-                    first_sem.at[kind, side], sem, to)
+                    first_sem.at[kind], sem, to)
 
     def second(kind, side, at, sem):
         lead, to = (((1 - y, x), across_y), ((y, 1 - x), across_x))[side]
         return send(sums[kind].at[at(kind, lead, side)], seconds[kind].at[at(kind, (), side)],
-                    second_sem.at[kind, side], sem, to)
+                    second_sem.at[kind], sem, to)
 
     def chunk(k):
         return lambda kind, lead, side: index(kind, lead, side, k)
 
+    def span(k, n):
+        def at(kind, lead, side):
+            if kind == QO_:
+                return (pl.ds(k, n),) + lead + (pl.ds(HALF_R * side, HALF_R),)
+            half, step = ((HALF_R, SUB), None, (HALF_DC, D_STEP))[kind]
+            return lead + (pl.ds(half * side + step * k, step * n),)
+        return at
+
+    def own_ring(kind, side, k):
+        return own_sem.at[side, lax.rem(kind * STEPS + k, SLOTS)]
+
+    def peer_ring(kind, side, k):
+        return peer_sem.at[side, lax.rem(kind * STEPS + k, 2 * SLOTS)]
+
     def load(kind, k, side, away):
         if away:
-            dst, sem, c = peers[kind], peer_sem.at[kind, side, k], 1 - core
+            dst, sem, c = peers[kind], peer_ring(kind, side, k), 1 - core
             copy = lambda a, b: send(a, b, push_sem.at[kind], sem, mate)
         else:
-            dst, sem, c = owns[kind], own_sem.at[kind, side, k], core
+            dst, sem, c = owns[kind], own_ring(kind, side, k), core
             copy = lambda a, b: pltpu.make_async_copy(a, b, sem)
         if kind == U_:
             at = index(kind, (), side, k)
@@ -187,8 +201,8 @@
         else:
             at = index(kind, (every, every), side, k)
             here, there = owns[kind].at[at], peers[kind].at[at]
-        pltpu.make_async_copy(here, here, own_sem.at[kind, side, k]).wait()
-        send(there, there, push_sem.at[kind], peer_sem.at[kind, side, k], mate).wait_recv()
+        pltpu.make_async_copy(here, here, own_ring(kind, side, k)).wait()
+        send(there, there, push_sem.at[kind], peer_ring(kind, side, k), mate).wait_recv()
 
     smalls = [(vrq, r_q), (vro, r_o), (vru, r_u), (vrd, r_d),
               (vcq, c_q), (vco, c_o), (vcu, c_u), (vcd, c_d), (vv, vv_in)]
@@ -219,7 +233,7 @@
     for side in range(2):
         staged[side].wait()
         send(stage.at[side], peer_u.at[index(U_, (every, every), side, 0)],
-             push_sem.at[U_], peer_sem.at[U_, side, 0], mate).start()
+             push_sem.at[U_], peer_ring(U_, side, 0), mate).start()
     vec_copy.start()
     for copy in small_copies:
         copy.start()
@@ -255,7 +269,7 @@
                     for b in range(4):
                         at = index(kind, (b // 2, b % 2), side, k)
                         owns[kind][at] = owns[kind][at] + peers[kind][at]
-                first(kind, side, chunk(k), a_sem.at[kind, side, k]).start()
+                first(kind, side, chunk(k), a_sem.at[kind, side, k // BATCH]).start()
                 if opening:
                     for step in OPENING[side]:
                         start_kind(U_, step, False)
@@ -275,6 +289,12 @@
 
     for copy in small_copies:
         copy.wait()
+    kept = [(wq, wq_out), (wo, wo_out), (wu, wu_out), (wd, wd_out), (wv, wv_out),
+            (mq, mq_out), (mo, mo_out), (mu, mu_out), (md, md_out), (mv, mv_out)]
+    kept = [pltpu.make_async_copy(a, b, small_sem.at[i]) for i, (a, b) in enumerate(kept)]
+    for copy in kept:
+        copy.start()
+
     for ref in (cs_qo, cs_u, rs_d, rp_acc, rpd_acc, p_q, p_o):
         ref[...] = jnp.zeros_like(ref)
     old = to_tiles(r_q[...], 0) + to_tiles(r_o[...], ROW_TILES) + to_tiles(r_u[...], 2 * ROW_TILES)
@@ -293,68 +313,73 @@
         pl.semaphore_wait(round_sem.at[i], beside)
 
     def stage2(kind):
-        def body(k, _):
+        for g, (k0, n) in enumerate(BATCHES):
             for side in range(2):
-                first(kind, side, chunk(k), a_sem.at[kind, side, k]).wait_recv()
+                first(kind, side, span(k0, n), a_sem.at[kind, side, g]).wait_recv()
                 lead, mine = (((1 - y, x), 1 - y), ((y, 1 - x), 1 - x))[side]
-                at = index(kind, lead, side, k)
-                sums[kind][at] = sums[kind][at] + firsts[kind][index(kind, (mine,), side, k)]
-                second(kind, side, chunk(k), b_sem.at[kind, side, k]).start()
-            return _
-        return body
+
+                def add(k, _):
+                    at = index(kind, lead, side, k)
+                    sums[kind][at] = sums[kind][at] + firsts[kind][index(kind, (mine,), side, k)]
+                    return _
+
+                lax.fori_loop(k0, k0 + n, add, 0)
+            for b, (k1, m) in enumerate(SECOND[kind]):
+                if k0 <= k1 < k0 + n:
+                    for side in range(2):
+                        second(kind, side, span(k1, m), b_sem.at[side, SECOND_AT[kind] + b]).start()
 
     for kind in (U_, QO_):
-        lax.fori_loop(0, STEPS, stage2(kind), 0)
+        stage2(kind)
     vec_x.wait_recv()
     vec_mid[1] = vec_mid[0] + vec_in[1]
     vec_y.start()
-    lax.fori_loop(0, STEPS, stage2(D_), 0)
+    stage2(D_)
 
     def finished(kind, side, k):
-        second(kind, side, chunk(k), b_sem.at[kind, side, k]).wait_recv()
         return (sums[kind][index(kind, (y, x), side, k)]
                 + firsts[kind][index(kind, ((y, x)[side],), side, k)]
                 + seconds[kind][index(kind, (), side, k)])
 
-    def stage3_u(k, _):
-        for side in range(2):
-            full = finished(U_, side, k)
-            hu[index(U_, (), side, k)] = full
-            sq = full * full
-            cs_u[...] += sq
-            row = jnp.sum(sq, axis=1, keepdims=True)
-            rp_acc[...] = jnp.where(lane == 2 * ROW_TILES + STEPS * side + k, row, rp_acc[...])
-        return _
-
-    def stage3_qo(k, _):
-        for side in range(2):
-            rows = pl.ds(HALF_R * side, HALF_R)
-            full = finished(QO_, side, k)
-            hqo[rows, pl.ds(pl.multiple_of(LANE * k, LANE), LANE)] = full
-            sq = full * full
-            in_q = lanes(sq.shape) + LANE * k < COLS[0]
-            p_q[rows, :] += jnp.where(in_q, sq, 0.0)
-            p_o[rows, :] += jnp.where(in_q, 0.0, sq)
-            part = sq[:SUB]
-            for t in range(1, STEPS):
-                part = part + sq[SUB * t:SUB * t + SUB]
-            cs_qo[k] += part
-        return _
-
-    def stage3_d(k, _):
-        for side in range(2):
-            full = finished(D_, side, k)
-            hd[index(D_, (), side, k)] = full
-            sq = full * full
-            both = rpd_acc[...]
-            for t in range(D_STEP // SUB):
-                part = sq[SUB * t:SUB * t + SUB]
-                rs_d[...] += part
-                col = jnp.sum(part, axis=1, keepdims=True)
-                at = (HALF_DC * side + D_STEP * k) // SUB + t
-                both = jnp.where(lane == at, col, both)
-            rpd_acc[...] = both
-        return _
+    def stage3_u(side, k):
+        full = finished(U_, side, k)
+        hu[index(U_, (), side, k)] = full
+        sq = full * full
+        cs_u[...] += sq
+        row = jnp.sum(sq, axis=1, keepdims=True)
+        rp_acc[...] = jnp.where(lane == 2 * ROW_TILES + STEPS * side + k, row, rp_acc[...])
+
+    def stage3_qo(side, k):
+        rows = pl.ds(HALF_R * side, HALF_R)
+        full = finished(QO_, side, k)
+        hqo[rows, pl.ds(pl.multiple_of(LANE * k, LANE), LANE)] = full
+        sq = full * full
+        in_q = lanes(sq.shape) + LANE * k < COLS[0]
+        p_q[rows, :] += jnp.where(in_q, sq, 0.0)
+        p_o[rows, :] += jnp.where(in_q, 0.0, sq)
+        part = sq[:SUB]
+        for t in range(1, STEPS):
+            part = part + sq[SUB * t:SUB * t + SUB]
+        cs_qo[k] += part
+
+    def stage3_d(side, k):
+        full = finished(D_, side, k)
+        hd[index(D_, (), side, k)] = full
+        sq = full * full
+        both = rpd_acc[...]
+        for t in range(D_STEP // SUB):
+            part = sq[SUB * t:SUB * t + SUB]
+            rs_d[...] += part
+            col = jnp.sum(part, axis=1, keepdims=True)
+            at = (HALF_DC * side + D_STEP * k) // SUB + t
+            both = jnp.where(lane == at, col, both)
+        rpd_acc[...] = both
+
+    def stage3(kind, take):
+        for b, (k0, n) in enumerate(SECOND[kind]):
+            for side in range(2):
+                second(kind, side, span(k0, n), b_sem.at[side, SECOND_AT[kind] + b]).wait_recv()
+                lax.fori_loop(k0, k0 + n, lambda k, _: [take(side, k), _][1], 0)
 
     def to_group(buf, at, i, n, axis, here):
         for d in range(1, n):
@@ -376,8 +401,8 @@
             out = out + buf[d]
         return out
 
-    lax.fori_loop(0, STEPS, stage3_u, 0)
-    lax.fori_loop(0, STEPS, stage3_qo, 0)
+    stage3(U_, stage3_u)
+    stage3(QO_, stage3_qo)
     vec_y.wait_recv()
     vec = vec_mid[1] + vec_in[2]
     hv[...] = vec
@@ -398,7 +423,7 @@
     for m in range(3):
         pack = jnp.where(lane1 == m, total(jnp.where(masks[m], rp, 0.0)), pack)
 
-    lax.fori_loop(0, STEPS, stage3_d, 0)
+    stage3(D_, stage3_d)
     rs = rs_d[...]
     s_all[linear] = jnp.where(lane1 == 3, total(rs), pack)
     to_all(s_all, 4)
@@ -504,12 +529,13 @@
     n_cd[...] = from_tiles(cold_new, 0, DC)
 
     for kind in range(3):
-        send(peers[kind], peers[kind], push_sem.at[kind], peer_sem.at[kind, 0, 0], mate).wait_send()
-        for side in range(2):
-            first(kind, side, whole, a_sem.at[kind, side, 0]).wait_send()
-            second(kind, side, whole, b_sem.at[kind, side, 0]).wait_send()
+        send(peers[kind], peers[kind], push_sem.at[kind], peer_sem.at[0, 0], mate).wait_send()
+        send(firsts[kind], firsts[kind], first_sem.at[kind], a_sem.at[kind, 0, 0], mate).wait_send()
+        send(seconds[kind], seconds[kind], second_sem.at[kind], b_sem.at[0, 0], mate).wait_send()
     for copy in (vec_core, vec_x, vec_y):
         copy.wait_send()
+    for copy in kept:
+        copy.wait()
     groups = ((rp_all, TP), (cs_all, FSDP), (rsd_all, TP), (rpd_all, FSDP), (s_all, DEVICES), (u_all, DEVICES))
     for i, (buf, n) in enumerate(groups):
         if i < len(groups) - 1:
@@ -529,8 +555,8 @@
 
 
 def update_kernel(*refs):
-    (hqo, hu, hd, hv, inv, vrq, vro, vru, vrd, vcq, vco, vcu, vcd, vv,
-     wq, wo, wu, wd, wv, mq, mo, mu, md, mv,
+    (hqo, hu, hd, hv, inv, wq, wo, wu, wd, wv, mq, mo, mu, md, mv,
+     vrq, vro, vru, vrd, vcq, vco, vcu, vcd, vv,
      wq_out, wo_out, wu_out, wd_out, wv_out, mq_out, mo_out, mu_out, md_out, mv_out,
      vrq_out, vcq_out, vro_out, vco_out, vru_out, vcu_out, vrd_out, vcd_out, vv_out,
      bwq, bwo, bwu, bwd, bmq, bmo, bmu, bmd, bwv, bmv, out_sem, small_sem) = refs
@@ -553,7 +579,7 @@
     stores.append(pltpu.make_async_copy(bmv, mv_out, small_sem.at[len(passed) + 1]))
     for copy in stores:
         copy.start()
-    for i, (m, r0, n) in enumerate(PIECES):
+    for m, r0, n in PIECES:
         scale = inv[:, m:m + 1]
         buf, c0 = held[m]
 
@@ -565,8 +591,10 @@
             m_buf[m][rows, :] = m_new
         rows = pl.ds(r0, n)
         for j, (src, dst) in enumerate(((w_buf, w_out), (m_buf, m_out))):
-            stores.append(pltpu.make_async_copy(src[m].at[rows, :], dst[m].at[rows, :], out_sem.at[i, j]))
-            stores[-1].start()
+            pltpu.make_async_copy(src[m].at[rows, :], dst[m].at[rows, :], out_sem.at[m, j]).start()
+    for m in range(4):
+        for j, (src, dst) in enumerate(((w_buf, w_out), (m_buf, m_out))):
+            stores.append(pltpu.make_async_copy(src[m], dst[m], out_sem.at[m, j]))
     for copy in stores:
         copy.wait()
 
@@ -601,35 +629,37 @@
         (1, WIDE), (1, DR),
         (FSDP, 1, WIDE), (TP, SUB, LANE), (TP, 1, DR), (FSDP, SUB, LANE),
         (DEVICES, 1, LANE), (DEVICES, 1, LANE)]
-    sems = [(3, 2, STEPS)] * 2 + [(3,), (3, 2), (3, 2)] + [(3, 2, STEPS)] * 2 + [(1,), (3,), (3,), (9,), (6,), (6,), (2,)]
+    sems = [(2, SLOTS), (2, 2 * SLOTS), (3,), (3,), (3,), (3, 2, len(BATCHES)),
+            (2, SECOND_AT[-1] + len(SECOND[-1])), (1,), (3,), (3,), (10,), (6,), (6,), (2,)]
+    ws = [w_qkv[0], w_out[0], w_up[0], w_down[0].T, w_vec]
+    ms = [m_qkv[0], m_out[0], m_up[0], m_down[0].T, m_vec]
+    mats = list(zip(*HELD))
+    state = [f32(*s) for s in mats + [vec]] + [jax.ShapeDtypeStruct(s, BF16) for s in mats + [vec]]
     inputs = [pltpu.with_memory_space_constraint(a, pltpu.HBM)
               for a in (g_qkv[0, 0].T, g_out[0, 0].T, g_up.reshape(2, 2, 2, R, UP), g_down[0, 0].T, g_vec[0],
-                        vr_qkv, vr_out, vr_up, vr_down, vc_qkv, vc_out, vc_up, vc_down, v_vec)]
+                        vr_qkv, vr_out, vr_up, vr_down, vc_qkv, vc_out, vc_up, vc_down, v_vec, *ws, *ms)]
     reduced = pl.pallas_call(
         reduce_kernel,
         name="reduce_and_scale",
-        out_shape=[f32(*s) for s in h_shapes + [vec, (1, LANE)] + rows_shapes + cols_shapes + [vec]],
-        in_specs=[IN_HBM] * 14,
-        out_specs=[IN_VMEM] * 14,
+        out_shape=([f32(*s) for s in h_shapes + [vec, (1, LANE)]] + state
+                   + [f32(*s) for s in rows_shapes + cols_shapes + [vec]]),
+        in_specs=[IN_HBM] * 24,
+        out_specs=[IN_VMEM] * 24,
         scratch_shapes=[vmem(*s) for s in shapes] + [dma(s) for s in sems] + [pltpu.SemaphoreType.REGULAR((TP + 1,))],
         compiler_params=pltpu.CompilerParams(
             collective_id=0, has_side_effects=True, vmem_limit_bytes=A_MIB * MIB),
     )(*inputs)
 
-    ws = [w_qkv[0], w_out[0], w_up[0], w_down[0].T, w_vec]
-    ms = [m_qkv[0], m_out[0], m_up[0], m_down[0].T, m_vec]
-    mats = list(zip(*HELD))
     outs = pl.pallas_call(
         update_kernel,
         name="update",
-        out_shape=([f32(*s) for s in mats + [vec]] + [jax.ShapeDtypeStruct(s, BF16) for s in mats + [vec]]
-                   + [f32(*s) for m in range(4) for s in (rows_shapes[m], cols_shapes[m])] + [f32(*vec)]),
+        out_shape=(state + [f32(*s) for m in range(4) for s in (rows_shapes[m], cols_shapes[m])] + [f32(*vec)]),
         in_specs=[IN_VMEM] * 24,
         out_specs=[IN_HBM] * 19,
         scratch_shapes=([vmem(*s) for s in mats] + [pltpu.VMEM(s, BF16) for s in mats]
-                        + [vmem(*vec), pltpu.VMEM(vec, BF16), dma((len(PIECES), 2)), dma((11,))]),
+                        + [vmem(*vec), pltpu.VMEM(vec, BF16), dma((4, 2)), dma((11,))]),
         compiler_params=pltpu.CompilerParams(vmem_limit_bytes=B_MIB * MIB),
-    )(*reduced, *ws, *ms)
+    )(*reduced)
     outs = list(outs)
     for i in range(10):
         if i % 5 == 3:

time: 126 us -> 124 us (0.984)
  Pallas kernels: 125 us -> 123 us
    pallas_call x1, Pallas kernels: 122 us -> 120 us  [local_step(): pl.pallas_call(reduce_kernel, name='reduce_and_scale', out_shape=[f32(*s)...]
where the time goes in v4:
time: 124 us
  Pallas kernels  123 us (99%)
    pallas_call x1, Pallas kernels, local_step(): pl.pallas_call(reduce_kernel, name='reduce_and_scale', out_shape=[f32(*s)...  120 us
    pallas_call x1, Pallas kernels, local_step(): pl.pallas_call(update_kernel, name='update', out_shape=state + [f32(*s) f...  2.7 us

profile of v4, /device:TPU:0, one launch (start us, length us, event | category | flops | bytes accessed | tf_op | source)
XLA Modules:
  0.0 123.7 jit_solution(5672627976572974822)
XLA Ops:
  0.7 120.3 %reduce_and_scale.1 = (f32[176,1408]{1,0:T(8,128)S(1)}, f32[176,1536]{1,0:T(8,128)S(1)}, f32[352,768]{1,0:T(8,128)S(1)}, f32[1,4704]{1,0:T(1,128)S(1)}, f32[1,12...) custom-call(f32[1056,1408]{1,0:T(8,128)} %bitcast.37, ...), custom_call_target="tpu_custom_call" | custom-call | tf_op jit(solution)/shard_map/reduce_and_scale/pallas_call | solution.py:641
  121.0 2.7 %update.1 = (f32[176,1056]{1,0:T(8,128)}, f32[176,352]{1,0:T(8,128)}, f32[176,1536]{1,0:T(8,128)}, f32[352,768]{1,0:T(8,128)}, f32[1,4704]{1,0:T(1,128)}, /*inde...) custom-call(f32[176,1408]{1,0:T(8,128)S(1)} %get-tuple-element.62.re, ...), custom_call_target="tpu_custom_call" | custom-call | tf_op jit(solution)/shard_map/update/pallas_call | solution.py:653

commit v5 on v4

--- a/solution.py
+++ b/solution.py
@@ -32,13 +32,14 @@
 ROW_TILES = R // SUB
 D_TILES = DC // SUB
 WIDE = -(-(QO + UP) // (SUB * LANE)) * SUB * LANE
-LOOK, SLOTS = 2, 3
-OPENING = ((1,), (2,))
+LOOK, SLOTS = 1, 2
+OPENING = ((1,), ())
 U_, QO_, D_ = 0, 1, 2
-BATCH = 6
-BATCHES = ((0, 6), (6, 5))
-SECOND = (BATCHES, BATCHES, ((0, 6), (6, 3), (9, 1), (10, 1)))
-SECOND_AT = (0, 2, 4)
+BATCH = 11
+BATCHES = ((0, 11),)
+SECOND = (BATCHES, BATCHES, ((0, 6), (6, 4), (10, 1)))
+SECOND_AT = (0, 1, 2)
+PARTS = ((0, 0), (1, 0), (0, 1), (1, 1))
 VR_AT, VEC_AT = 4, 8
 
 
@@ -94,7 +95,7 @@
      p_q, p_o, cs_qo, cs_u, rs_d, rp_acc, rpd_acc, rp_old, rpd_old, col_buf, rowd_buf,
      cs_all, rp_all, rsd_all, rpd_all, s_all, u_all,
      own_sem, peer_sem, push_sem, first_sem, second_sem, a_sem, b_sem,
-     vec_sem, vec_send, vec_recv, small_sem, stat_send, stat_recv, stage_sem, round_sem) = refs
+     vec_send, vec_recv, stat_send, stat_recv, open_sem, round_sem) = refs
 
     me = lax.axis_index("fsdp")
     z = lax.axis_index("tp")
@@ -152,6 +153,12 @@
             half, step = ((HALF_R, SUB), None, (HALF_DC, D_STEP))[kind]
             return lead + (pl.ds(half * side + step * k, step * n),)
         return at
+
+    def opened(i):
+        side, stays = PARTS[i]
+        lead = (((every, 1 - x), (every, x)), ((1 - y, every), (y, every)))[side][stays]
+        return send(stage.at[(side,) + lead], peer_u.at[index(U_, lead, side, 0)],
+                    push_sem.at[U_], open_sem.at[side] if stays else peer_ring(U_, side, 0), mate)
 
     def own_ring(kind, side, k):
         return own_sem.at[side, lax.rem(kind * STEPS + k, SLOTS)]
@@ -206,11 +213,12 @@
 
     smalls = [(vrq, r_q), (vro, r_o), (vru, r_u), (vrd, r_d),
               (vcq, c_q), (vco, c_o), (vcu, c_u), (vcd, c_d), (vv, vv_in)]
-    small_copies = [pltpu.make_async_copy(a, b, small_sem.at[i]) for i, (a, b) in enumerate(smalls)]
-    vec_copy = pltpu.make_async_copy(gv, vec_own, vec_sem.at[0])
+    spare = [stat_send.at[i] for i in range(6)] + [second_sem.at[i] for i in range(3)] + [vec_send.at[2]]
+    small_copies = [pltpu.make_async_copy(a, b, sem) for (a, b), sem in zip(smalls, spare)]
+    vec_copy = pltpu.make_async_copy(gv, vec_own, vec_send.at[0])
 
     staged = [pltpu.make_async_copy(gu.at[(every, every, 1 - core) + index(U_, (), side, 0)],
-                                    stage.at[side], stage_sem.at[side]) for side in range(2)]
+                                    stage.at[side], push_sem.at[(QO_, D_)[side]]) for side in range(2)]
     for copy in staged:
         copy.start()
     start_kind(U_, 0, False)
@@ -230,10 +238,10 @@
     signal_z(barrier)
     pl.semaphore_wait(barrier, len(near) + beside)
 
-    for side in range(2):
-        staged[side].wait()
-        send(stage.at[side], peer_u.at[index(U_, (every, every), side, 0)],
-             push_sem.at[U_], peer_ring(U_, side, 0), mate).start()
+    for copy in staged:
+        copy.wait()
+    for i, (side, part) in enumerate(PARTS):
+        opened(i).start()
     vec_copy.start()
     for copy in small_copies:
         copy.start()
@@ -254,11 +262,10 @@
                     first_row = start - R * (2 * b + which)
                     s_qo[k, b // 2, b % 2, pl.ds(first_row, stop - start), :] = turned[start - lo:stop - lo]
 
-    def stage1(kind, opening=False):
+    def stage1(kind):
         def body(k, _):
-            if not opening:
-                start_loads(k + kind * STEPS + LOOK, False)
-                start_loads(k + kind * STEPS + LOOK, True)
+            start_loads(k + kind * STEPS + LOOK, False)
+            start_loads(k + kind * STEPS + LOOK, True)
             if kind == QO_:
                 loaded(kind, 0, k)
                 for which in range(2):
@@ -270,14 +277,23 @@
                         at = index(kind, (b // 2, b % 2), side, k)
                         owns[kind][at] = owns[kind][at] + peers[kind][at]
                 first(kind, side, chunk(k), a_sem.at[kind, side, k // BATCH]).start()
-                if opening:
-                    for step in OPENING[side]:
-                        start_kind(U_, step, False)
-                        start_kind(U_, step, True)
             return _
         return body
 
-    stage1(U_, True)(0, 0)
+    for side in range(2):
+        at = index(U_, (every, every), side, 0)
+        pltpu.make_async_copy(own_u.at[at], own_u.at[at], own_ring(U_, side, 0)).wait()
+    for i, (side, stays) in enumerate(PARTS):
+        opened(i).wait_recv()
+        for b in range(2):
+            lead = (((b, 1 - x), (b, x)), ((1 - y, b), (y, b)))[side][stays]
+            at = index(U_, lead, side, 0)
+            own_u[at] = own_u[at] + peer_u[at]
+        if not stays:
+            first(U_, side, chunk(0), a_sem.at[U_, side, 0]).start()
+            for step in OPENING[side]:
+                start_kind(U_, step, False)
+                start_kind(U_, step, True)
     vec_copy.wait()
     vec_core.start()
     lax.fori_loop(1, STEPS, stage1(U_), 0)
@@ -291,7 +307,7 @@
         copy.wait()
     kept = [(wq, wq_out), (wo, wo_out), (wu, wu_out), (wd, wd_out), (wv, wv_out),
             (mq, mq_out), (mo, mo_out), (mu, mu_out), (md, md_out), (mv, mv_out)]
-    kept = [pltpu.make_async_copy(a, b, small_sem.at[i]) for i, (a, b) in enumerate(kept)]
+    kept = [pltpu.make_async_copy(a, b, sem) for (a, b), sem in zip(kept, spare)]
     for copy in kept:
         copy.start()
 
@@ -304,6 +320,9 @@
     lane1 = lanes((1, LANE))
     masks = [jnp.logical_and(lane >= ROW_TILES * m, lane < ROW_TILES * (m + 1)) for m in range(3)]
     old_sums = [total(jnp.where(masks[m], old, 0.0)) for m in range(3)] + [total(r_d[...])]
+
+    for copy in kept:
+        copy.wait()
 
     for i, to in enumerate(near):
         signal(round_sem.at[i], to)
@@ -534,8 +553,6 @@
         send(seconds[kind], seconds[kind], second_sem.at[kind], b_sem.at[0, 0], mate).wait_send()
     for copy in (vec_core, vec_x, vec_y):
         copy.wait_send()
-    for copy in kept:
-        copy.wait()
     groups = ((rp_all, TP), (cs_all, FSDP), (rsd_all, TP), (rpd_all, FSDP), (s_all, DEVICES), (u_all, DEVICES))
     for i, (buf, n) in enumerate(groups):
         if i < len(groups) - 1:
@@ -549,7 +566,7 @@
     spread(u_all, len(groups) - 1, DEVICES).wait_send()
 
 
-PIECES = ((3, 0, 48), (3, 48, 128), (3, 176, 176), (2, 0, 96), (2, 96, 80), (0, 0, 96), (0, 96, 80), (1, 0, R))
+PIECES = ((3, 0, 96), (3, 96, 128), (3, 224, 128), (2, 0, 64), (2, 64, 64), (2, 128, 48), (0, 0, 96), (0, 96, 80), (1, 0, R))
 HELD = (ROWS[:3] + (DC,), COLS[:3] + (DR,))
 GROUP = 16
 
@@ -630,7 +647,7 @@
         (FSDP, 1, WIDE), (TP, SUB, LANE), (TP, 1, DR), (FSDP, SUB, LANE),
         (DEVICES, 1, LANE), (DEVICES, 1, LANE)]
     sems = [(2, SLOTS), (2, 2 * SLOTS), (3,), (3,), (3,), (3, 2, len(BATCHES)),
-            (2, SECOND_AT[-1] + len(SECOND[-1])), (1,), (3,), (3,), (10,), (6,), (6,), (2,)]
+            (2, SECOND_AT[-1] + len(SECOND[-1])), (3,), (3,), (6,), (6,), (2,)]
     ws = [w_qkv[0], w_out[0], w_up[0], w_down[0].T, w_vec]
     ms = [m_qkv[0], m_out[0], m_up[0], m_down[0].T, m_vec]
     mats = list(zip(*HELD))

time: 124 us -> 124 us (level)
  no operation moved by 1% of the time
where the time goes in v5:
time: 124 us; the launch traced here: 123 us
  Pallas kernels  122 us (98%)
    pallas_call x1, Pallas kernels, local_step(): pl.pallas_call(reduce_kernel, name='reduce_and_scale', out_shape=[f32(*s)...  120 us
    pallas_call x1, Pallas kernels, local_step(): pl.pallas_call(update_kernel, name='update', out_shape=state + [f32(*s) f...  2.63 us

profile of v5, /device:TPU:0, one launch (start us, length us, event | category | flops | bytes accessed | tf_op | source)
XLA Modules:
  0.0 123.1 jit_solution(283431709233992392)
XLA Ops:
  0.7 119.8 %reduce_and_scale.1 = (f32[176,1408]{1,0:T(8,128)S(1)}, f32[176,1536]{1,0:T(8,128)S(1)}, f32[352,768]{1,0:T(8,128)S(1)}, f32[1,4704]{1,0:T(1,128)S(1)}, f32[1,12...) custom-call(f32[1056,1408]{1,0:T(8,128)} %bitcast.37, ...), custom_call_target="tpu_custom_call" | custom-call | tf_op jit(solution)/shard_map/reduce_and_scale/pallas_call | solution.py:658
  120.5 2.6 %update.1 = (f32[176,1056]{1,0:T(8,128)}, f32[176,352]{1,0:T(8,128)}, f32[176,1536]{1,0:T(8,128)}, f32[352,768]{1,0:T(8,128)}, f32[1,4704]{1,0:T(1,128)}, /*inde...) custom-call(f32[176,1408]{1,0:T(8,128)S(1)} %get-tuple-element.62.re, ...), custom_call_target="tpu_custom_call" | custom-call | tf_op jit(solution)/shard_map/update/pallas_call | solution.py:670

commit v6 on v5

--- a/solution.py
+++ b/solution.py
@@ -32,8 +32,8 @@
 ROW_TILES = R // SUB
 D_TILES = DC // SUB
 WIDE = -(-(QO + UP) // (SUB * LANE)) * SUB * LANE
-LOOK, SLOTS = 1, 2
-OPENING = ((1,), ())
+LOOK, SLOTS = 2, 3
+OPENING = ((1,), (2,))
 U_, QO_, D_ = 0, 1, 2
 BATCH = 11
 BATCHES = ((0, 11),)

time: 124 us -> 123 us (level)
  no operation moved by 1% of the time
where the time goes in v6:
time: 123 us
  Pallas kernels  122 us (99%)
    pallas_call x1, Pallas kernels, local_step(): pl.pallas_call(reduce_kernel, name='reduce_and_scale', out_shape=[f32(*s)...  120 us
    pallas_call x1, Pallas kernels, local_step(): pl.pallas_call(update_kernel, name='update', out_shape=state + [f32(*s) f...  2.63 us

profile of v6, /device:TPU:0, one launch (start us, length us, event | category | flops | bytes accessed | tf_op | source)
XLA Modules:
  0.0 123.2 jit_solution(4403939179517019749)
XLA Ops:
  0.7 119.9 %reduce_and_scale.1 = (f32[176,1408]{1,0:T(8,128)S(1)}, f32[176,1536]{1,0:T(8,128)S(1)}, f32[352,768]{1,0:T(8,128)S(1)}, f32[1,4704]{1,0:T(1,128)S(1)}, f32[1,12...) custom-call(f32[1056,1408]{1,0:T(8,128)} %bitcast.37, ...), custom_call_target="tpu_custom_call" | custom-call | tf_op jit(solution)/shard_map/reduce_and_scale/pallas_call | solution.py:658
  120.5 2.6 %update.1 = (f32[176,1056]{1,0:T(8,128)}, f32[176,352]{1,0:T(8,128)}, f32[176,1536]{1,0:T(8,128)}, f32[352,768]{1,0:T(8,128)}, f32[1,4704]{1,0:T(1,128)}, /*inde...) custom-call(f32[176,1408]{1,0:T(8,128)S(1)} %get-tuple-element.62.re, ...), custom_call_target="tpu_custom_call" | custom-call | tf_op jit(solution)/shard_map/update/pallas_call | solution.py:670
